TPU v7x, 32 devices: a whole 2x2x4 slice. The times are simulated.
32 devices in a mesh: rep: 4 (over x, y), dp: 8 (over z, core).
Axes of the slice: x: 2, y: 2, z: 4, core: 2. Of those that a mesh axis runs over, the one named last changes fastest.
Arguments:
- x: bfloat16 [32, 4096, 512], P(('rep', 'dp')), parts along dimension 0
- dy: bfloat16 [32, 4096, 512], P(('rep', 'dp')), parts along dimension 0
- w_gate: bfloat16 [2, 512, 1408], P(None, 'dp')
- w_up: bfloat16 [2, 512, 1408], P(None, 'dp')
- w_down: bfloat16 [2, 1408, 512], P(None, 'dp')
Outputs:
- output 1: bfloat16 [32, 4096, 512], P(('rep', 'dp')), parts along dimension 0
- output 2: bfloat16 [8, 512, 1408], P('rep', 'dp'), parts along dimension 0
- output 3: bfloat16 [8, 512, 1408], P('rep', 'dp'), parts along dimension 0
- output 4: bfloat16 [8, 1408, 512], P('rep', 'dp'), parts along dimension 0
There are 4 independent parts. A program takes and returns all parts, laid end to end along the dimension named above; an argument that names none is the same for every part.
All inputs are finite; a program needn't handle non-finite values.
Results may differ from a plain program's by a relative error of at most 0.018.
Values are sent between devices in bfloat16 or wider.
A program may use at most 2 GiB of HBM per device.

v0:
```python
import functools

import jax
import jax.numpy as jnp
from jax import lax
from jax.experimental import pallas as pl
from jax.experimental.pallas import tpu as pltpu
from jax.sharding import PartitionSpec as P

EPS = 1e-6
BF, F32 = jnp.bfloat16, jnp.float32
TM = 512
CH = 256
VMEM_LIMIT = 60 * 2**20


def dot(a, b):
    return jnp.dot(a, b, preferred_element_type=F32)


def dot_nt(a, b):
    return lax.dot_general(a, b, (((1,), (1,)), ((), ())), preferred_element_type=F32)


def chunks(ff):
    return [(s, min(CH, ff - s)) for s in range(0, ff, CH)]


def joined(gate, up):
    return jnp.concatenate([t[:, s : s + w] for s, w in chunks(gate.shape[1]) for t in (gate, up)], axis=1)


def parted(t):
    ff = t.shape[1] // 2
    gate = jnp.concatenate([t[:, 2 * s : 2 * s + w] for s, w in chunks(ff)], axis=1)
    up = jnp.concatenate([t[:, 2 * s + w : 2 * (s + w)] for s, w in chunks(ff)], axis=1)
    return gate, up


def scale_of(wide):
    return lax.rsqrt(jnp.mean(wide * wide, -1, keepdims=True) + EPS)


def sigmoid(t):
    return 0.5 * jnp.tanh(0.5 * t) + 0.5


def forward_kernel(h_ref, w1_ref, w2_ref, o_ref, p_ref):
    ff = w2_ref.shape[0]
    wide = h_ref[...].astype(F32)
    a = (wide * scale_of(wide)).astype(BF)
    for s, w in chunks(ff):
        gu = dot(a, w1_ref[:, 2 * s : 2 * (s + w)])
        gate, up = gu[:, :w], gu[:, w:]
        p_ref[:, s : s + w] = (gate * sigmoid(gate) * up).astype(BF)
    o_ref[...] = h_ref[...] + dot(p_ref[...], w2_ref[...]).astype(BF)


def hidden_kernel(h_ref, by_ref, w1_ref, w2_ref, dgu_ref, at_ref, dw2_ref, p_ref, acc_ref):
    ff = w2_ref.shape[0]
    step = pl.program_id(0)
    wide = h_ref[...].astype(F32)
    a = (wide * scale_of(wide)).astype(BF)
    at_ref[...] = a.T
    by = by_ref[...]
    for s, w in chunks(ff):
        gu = dot(a, w1_ref[:, 2 * s : 2 * (s + w)])
        dp = dot_nt(by, w2_ref[s : s + w, :]).astype(BF).astype(F32)
        gate, up = gu[:, :w], gu[:, w:]
        sg = sigmoid(gate)
        silu = gate * sg
        p_ref[:, s : s + w] = (silu * up).astype(BF)
        dgu_ref[:, 2 * s : 2 * s + w] = (dp * up * (sg + silu * (1 - sg))).astype(BF)
        dgu_ref[:, 2 * s + w : 2 * (s + w)] = (dp * silu).astype(BF)
    term = dot(by.T, p_ref[...])

    @pl.when(step == 0)
    def _():
        acc_ref[...] = term

    @pl.when(step > 0)
    def _():
        acc_ref[...] += term

    @pl.when(step == pl.num_programs(0) - 1)
    def _():
        dw2_ref[...] = acc_ref[...].astype(BF).T


def weights_kernel(at_ref, dgu_ref, dw1_ref):
    dw1_ref[...] = dot(at_ref[...], dgu_ref[...]).astype(BF)


def input_kernel(h_ref, by_ref, dgu_ref, w1_ref, o_ref):
    da = dot_nt(dgu_ref[...], w1_ref[...]).astype(BF).astype(F32)
    wide = h_ref[...].astype(F32)
    scale = scale_of(wide)
    inner = jnp.mean(da * wide, -1, keepdims=True)
    o_ref[...] = by_ref[...] + (scale * da - (scale * scale * scale * inner) * wide).astype(BF)


def params():
    return pltpu.CompilerParams(dimension_semantics=("arbitrary",), vmem_limit_bytes=VMEM_LIMIT)


def cost(flops, nbytes):
    return pl.CostEstimate(flops=flops, bytes_accessed=nbytes, transcendentals=0)


def whole(shape):
    return pl.BlockSpec(shape, lambda i: (0,) * len(shape))


def rows(width):
    return pl.BlockSpec((TM, width), lambda i: (i, 0))


def forward(h, w1, w2):
    t, d = h.shape
    ff = w2.shape[0]
    return pl.pallas_call(
        forward_kernel, grid=(t // TM,), name="forward",
        in_specs=[rows(d), whole(w1.shape), whole(w2.shape)], out_specs=rows(d),
        out_shape=jax.ShapeDtypeStruct((t, d), BF), scratch_shapes=[pltpu.VMEM((TM, ff), BF)],
        compiler_params=params(), cost_estimate=cost(6 * t * d * ff, 4 * t * d),
    )(h, w1, w2)


def hidden(h, by, w1, w2):
    t, d = h.shape
    ff = w2.shape[0]
    return pl.pallas_call(
        hidden_kernel, grid=(t // TM,), name="hidden",
        in_specs=[rows(d), rows(d), whole(w1.shape), whole(w2.shape)],
        out_specs=[rows(2 * ff), pl.BlockSpec((d, TM), lambda i: (0, i)), whole((ff, d))],
        out_shape=[jax.ShapeDtypeStruct(s, BF) for s in ((t, 2 * ff), (d, t), (ff, d))],
        scratch_shapes=[pltpu.VMEM((TM, ff), BF), pltpu.VMEM((d, ff), F32)],
        compiler_params=params(), cost_estimate=cost(8 * t * d * ff, 8 * t * d + 4 * t * ff),
    )(h, by, w1, w2)


def by_weights(at, dgu):
    d, t = at.shape
    n = dgu.shape[1]
    return pl.pallas_call(
        weights_kernel, grid=(n // 256,), name="by_weights",
        in_specs=[whole((d, t)), pl.BlockSpec((t, 256), lambda i: (0, i))],
        out_specs=pl.BlockSpec((d, 256), lambda i: (0, i)),
        out_shape=jax.ShapeDtypeStruct((d, n), BF),
        compiler_params=params(), cost_estimate=cost(2 * t * d * n, 2 * t * n + 2 * t * d),
    )(at, dgu)


def by_input(h, by, dgu, w1):
    t, d = h.shape
    n = dgu.shape[1]
    return pl.pallas_call(
        input_kernel, grid=(t // TM,), name="by_input",
        in_specs=[rows(d), rows(d), rows(n), whole(w1.shape)], out_specs=rows(d),
        out_shape=jax.ShapeDtypeStruct((t, d), BF),
        compiler_params=params(), cost_estimate=cost(2 * t * d * n, 2 * t * n + 6 * t * d),
    )(h, by, dgu, w1)


def gather(w):
    return lax.all_gather(w, "dp", axis=0, tiled=True)


def scatter(g):
    return lax.psum_scatter(g, "dp", scatter_dimension=0, tiled=True)


def solution(mesh):
    def step(x, dy, w_gate, w_up, w_down):
        x, by = x[0], dy[0]
        layers = w_gate.shape[0]
        w1 = [gather(joined(w_gate[n], w_up[n])) for n in range(layers)]
        w2 = [gather(w_down[n]) for n in range(layers)]
        states = [x]
        for n in range(layers - 1):
            states.append(forward(states[-1], w1[n], w2[n]))
        g1, g2 = [None] * layers, [None] * layers
        for n in reversed(range(layers)):
            dgu, at, dw2 = hidden(states[n], by, w1[n], w2[n])
            g2[n] = scatter(dw2)
            g1[n] = scatter(by_weights(at, dgu))
            by = by_input(states[n], by, dgu, w1[n])
        gates, ups = zip(*(parted(g) for g in g1))
        return by[None], jnp.stack(gates), jnp.stack(ups), jnp.stack(g2)

    spread, by_rows = P(("rep", "dp"), None, None), P(None, "dp", None)
    group = P("rep", "dp", None)
    return jax.shard_map(
        step, mesh=mesh, in_specs=(spread, spread, by_rows, by_rows, by_rows),
        out_specs=(spread, group, group, group), check_vma=False,
    )
```

profile of v0, /device:TPU:0, one launch (start us, length us, event | category | flops | bytes accessed | tf_op | source)
XLA Modules:
  0.0 358.6 jit_solution(67653268963012221)
XLA Ops:
  7.2 1.8 fusion
  9.0 1.0 slice_bitcast_fusion.1
  10.1 1.0 slice_bitcast_fusion
  13.8 23.3 %all-gather.11.cloned.1.call-done = bf16[1,1408,512]{2,1,0:T(8,128)(2,1)} async-done(((bf16[1,176,512]{2,1,0:T(8,128)(2,1)}), bf16[1,1408,512]{2,1,0:T(8,128)(2,1)}) %all-gather.11.cloned.1.call-update) | async-done | bytes 1441808 | tf_op jit(solution)/shard_map/all_gather | solution.py:166
  37.2 37.4 %all-gather.7.cloned.1.call-done.w1_ref = bf16[512,2816]{1,0:T(8,128)(2,1)} async-done(((bf16[64,2816]{1,0:T(8,128)(2,1)}), bf16[512,2816]{1,0:T(8,128)(2,1)}) %all-gather.7.cloned.1.call-update) | async-done | bytes 2883600 | tf_op jit(solution)/shard_map/all_gather | solution.py:166
  74.6 23.8 %forward.1.h_ref = bf16[4096,512]{1,0:T(8,128)(2,1)} custom-call(bf16[4096,512]{1,0:T(8,128)(2,1)} %bitcast.27, bf16[512,2816]{1,0:T(8,128)(2,1)} %all-gather.7.cloned.1.call-done.w1_ref, bf16[1408,512]{1,0:T(8,128)(2,1)} %bitcast.30), custom_call_target="tpu_custom_call" | custom-call | flops 17716740096 | bytes 8388608 | tf_op jit(solution)/shard_map/forward/pallas_call | solution.py:121
  98.4 1.9 all-gather.13.cloned.1.call-done
  100.2 37.3 %all-gather.9.cloned.1.call-done.w1_ref = bf16[512,2816]{1,0:T(8,128)(2,1)} async-done(((bf16[64,2816]{1,0:T(8,128)(2,1)}), bf16[512,2816]{1,0:T(8,128)(2,1)}) %all-gather.9.cloned.1.call-update) | async-done | bytes 2883600 | tf_op jit(solution)/shard_map/all_gather | solution.py:166
  137.5 35.7 %hidden.2 = (bf16[4096,2816]{1,0:T(8,128)(2,1)}, bf16[512,4096]{1,0:T(8,128)(2,1)}, bf16[1408,512]{1,0:T(8,128)(2,1)}) custom-call(bf16[4096,512]{1,0:T(8,128)(2,1)} %forward.1.h_ref, bf16[4096,512]{1,0:T(8,128)(2,1)} %bitcast.25, bf16[512,2816]{1,0:T(8,128)(2,1)} %all-gather.9.cloned.1.call-done.w1_ref, bf16[1408,512]{1,0:T(8,128)(2,1)} %bitcast.32), custom_call_target="tpu_custom_call" | custom-call | flops 23622320128 | bytes 39845888 | tf_op jit(solution)/shard_map/hidden/pallas_call | solution.py:132
  173.4 20.7 %by_input.2.by_ref = bf16[4096,512]{1,0:T(8,128)(2,1)} custom-call(bf16[4096,512]{1,0:T(8,128)(2,1)} %forward.1.h_ref, bf16[4096,512]{1,0:T(8,128)(2,1)} %bitcast.26, bf16[4096,2816]{1,0:T(8,128)(2,1)} %get-tuple-element.10.dgu_ref, bf16[512,2816]{1,0:T(8,128)(2,1)} %all-gather.9.cloned.1.call-done.w1_ref), custom_call_target="tpu_custom_call" | custom-call | flops 11811160064 | bytes 35651584 | tf_op jit(solution)/shard_map/by_input/pallas_call | solution.py:157
  194.2 35.7 %hidden.3 = (bf16[4096,2816]{1,0:T(8,128)(2,1)}, bf16[512,4096]{1,0:T(8,128)(2,1)}, bf16[1408,512]{1,0:T(8,128)(2,1)}) custom-call(bf16[4096,512]{1,0:T(8,128)(2,1)} %bitcast.28, bf16[4096,512]{1,0:T(8,128)(2,1)} %by_input.2.by_ref, bf16[512,2816]{1,0:T(8,128)(2,1)} %all-gather.7.cloned.1.call-done.w1_ref, bf16[1408,512]{1,0:T(8,128)(2,1)} %bitcast.31), custom_call_target="tpu_custom_call" | custom-call | flops 23622320128 | bytes 39845888 | tf_op jit(solution)/shard_map/hidden/pallas_call | solution.py:132
  229.9 19.8 %by_weights.3 = bf16[512,2816]{1,0:T(8,128)(2,1)} custom-call(bf16[512,4096]{1,0:T(8,128)(2,1)} %get-tuple-element.13.at_ref, bf16[4096,2816]{1,0:T(8,128)(2,1)} %get-tuple-element.10.dgu_ref), custom_call_target="tpu_custom_call" | custom-call | flops 11811160064 | bytes 27262976 | tf_op jit(solution)/shard_map/by_weights/pallas_call | solution.py:145
  249.8 19.8 %by_weights.2 = bf16[512,2816]{1,0:T(8,128)(2,1)} custom-call(bf16[512,4096]{1,0:T(8,128)(2,1)} %get-tuple-element.12.at_ref, bf16[4096,2816]{1,0:T(8,128)(2,1)} %get-tuple-element.11.dgu_ref), custom_call_target="tpu_custom_call" | custom-call | flops 11811160064 | bytes 27262976 | tf_op jit(solution)/shard_map/by_weights/pallas_call | solution.py:145
  269.6 20.7 %by_input.3 = bf16[4096,512]{1,0:T(8,128)(2,1)} custom-call(bf16[4096,512]{1,0:T(8,128)(2,1)} %bitcast.29, bf16[4096,512]{1,0:T(8,128)(2,1)} %by_input.2.by_ref, bf16[4096,2816]{1,0:T(8,128)(2,1)} %get-tuple-element.11.dgu_ref, bf16[512,2816]{1,0:T(8,128)(2,1)} %all-gather.7.cloned.1.call-done.w1_ref), custom_call_target="tpu_custom_call" | custom-call | flops 11811160064 | bytes 35651584 | tf_op jit(solution)/shard_map/by_input/pallas_call | solution.py:157
  290.3 1.8 pad_maximum_fusion.2
  292.0 10.1 %reduce-scatter.7.cloned.1.call-done = bf16[64,2816]{1,0:T(8,128)(2,1)} async-done(((bf16[512,2816]{1,0:T(8,128)(2,1)}), bf16[64,2816]{1,0:T(8,128)(2,1)}) %reduce-scatter.7.cloned.1.call-update) | async-done | bytes 360464 | tf_op jit(solution)/shard_map/reduce_scatter | solution.py:170
  302.9 39.4 %reduce-scatter.5.cloned.1.call-done = bf16[64,2816]{1,0:T(8,128)(2,1)} async-done(((bf16[512,2816]{1,0:T(8,128)(2,1)}), bf16[64,2816]{1,0:T(8,128)(2,1)}) %reduce-scatter.5.cloned.1.call-update) | async-done | bytes 360464 | tf_op jit(solution)/shard_map/reduce_scatter | solution.py:170
  343.0 0.8 constant_dynamic-update-slice_fusion.46
  343.8 0.8 constant_dynamic-update-slice_fusion.45
  344.6 0.8 constant_dynamic-update-slice_fusion.44
  345.4 0.8 constant_dynamic-update-slice_fusion.43
  346.9 0.8 constant_dynamic-update-slice_fusion.40
  347.7 0.8 constant_dynamic-update-slice_fusion.39
  350.8 0.9 pad_maximum_fusion
  (52 shorter events, 7.5 us)
Async XLA Ops:
  7.2 30.0 %all-gather.11.cloned.1.call-start = ((), (), s32[]{:S(2)}) async-start(), calls=%async_computation.10 | async-start | bytes 1622016 | tf_op jit(solution)/shard_map/all_gather | solution.py:166
  9.0 65.6 %all-gather.7.cloned.1.call-start = ((), (), s32[]{:S(2)}) async-start(), calls=%async_computation.4 | async-start | bytes 3244032 | tf_op jit(solution)/shard_map/all_gather | solution.py:166
  11.3 0.7 copy-start.1
  12.1 88.2 %all-gather.13.cloned.1.call-start = ((), (), s32[]{:S(2)}) async-start(), calls=%async_computation.11 | async-start | bytes 1622016 | tf_op jit(solution)/shard_map/all_gather | solution.py:166
  12.8 124.7 %all-gather.9.cloned.1.call-start = ((), (), s32[]{:S(2)}) async-start(), calls=%async_computation.5 | async-start | bytes 3244032 | tf_op jit(solution)/shard_map/all_gather | solution.py:166
  13.0 0.7 copy-start
  13.8 276.5 %reduce-scatter.11.cloned.1.call-start = ((), (), s32[]{:S(2)}) async-start(), calls=%async_computation.9 | async-start | bytes 1622016 | tf_op jit(solution)/shard_map/reduce_scatter | solution.py:170
  173.2 117.1 %reduce-scatter.9.cloned.1.call-start = ((), (), s32[]{:S(2)}) async-start(), calls=%async_computation.8 | async-start | bytes 1622016 | tf_op jit(solution)/shard_map/reduce_scatter | solution.py:170
  229.9 72.2 %reduce-scatter.7.cloned.1.call-start = ((), (), s32[]{:S(2)}) async-start(), calls=%async_computation.7 | async-start | bytes 3244032 | tf_op jit(solution)/shard_map/reduce_scatter | solution.py:170
  249.7 92.6 %reduce-scatter.5.cloned.1.call-start = ((), (), s32[]{:S(2)}) async-start(), calls=%async_computation.6 | async-start | bytes 3244032 | tf_op jit(solution)/shard_map/reduce_scatter | solution.py:170
Sparse Core Ops, SparseCore 0:
  10.2 26.9 all-gather.10
  39.4 35.1 all-gather.6
  76.8 23.3 all-gather.12
  102.3 35.1 all-gather.8
  173.3 32.9 reduce-scatter.10
  230.0 32.9 reduce-scatter.8
  265.3 36.7 reduce-scatter.6
  304.4 37.7 reduce-scatter.4
where the time goes:
time: 360 us; the launch traced here: 359 us
  Pallas kernels  176 us (49%)
  waiting for transfers between devices  150 us (42%)
  local copies, waits for them, and re-layouts  14.7 us (4%)
  between operations  14.3 us (4%)
    all_gather x4, waiting for transfers between devices, gather(): return lax.all_gather(w, 'dp', axis=0, tiled=True)  99.9 us
    pallas_call x2, Pallas kernels, hidden(): pl.pallas_call(hidden_kernel, grid=(t // TM,), name='hidden', in_specs=[r...  71.3 us
    reduce_scatter x4, waiting for transfers between devices, scatter(): return lax.psum_scatter(g, 'dp', scatter_dimension=0, tiled=True)  49.4 us
    pallas_call x2, Pallas kernels, by_input(): pl.pallas_call(input_kernel, grid=(t // TM,), name='by_input', in_specs=[...  41.4 us
    pallas_call x2, Pallas kernels, by_weights(): pl.pallas_call(weights_kernel, grid=(n // 256,), name='by_weights', in_sp...  39.5 us
    pallas_call x1, Pallas kernels, forward(): pl.pallas_call(forward_kernel, grid=(t // TM,), name='forward', in_specs=...  23.8 us
    unnamed x36, local copies, waits for them, and re-layouts  9.37 us
  transfers between devices with their start and end apart: 8, of which 6 were waited for; matrix products, arithmetic and copies ran while one was open for 1% of the time, Pallas kernels for 39%

commit v1 on v0

v1 whole, which is shorter than its diff:
```python
import functools

import jax
import jax.numpy as jnp
from jax import lax
from jax.experimental import pallas as pl
from jax.experimental.pallas import tpu as pltpu
from jax.sharding import PartitionSpec as P

EPS = 1e-6
BF, F32 = jnp.bfloat16, jnp.float32
TM = 512
CH = 256
VMEM_LIMIT = 60 * 2**20


def dot(a, b):
    return jnp.dot(a, b, preferred_element_type=F32)


def dot_nt(a, b):
    return lax.dot_general(a, b, (((1,), (1,)), ((), ())), preferred_element_type=F32)


def chunks(ff):
    return [(s, min(CH, ff - s)) for s in range(0, ff, CH)]


def joined(gate, up):
    return jnp.concatenate([t[:, s : s + w] for s, w in chunks(gate.shape[1]) for t in (gate, up)], axis=1)


def parted(t):
    ff = t.shape[1] // 2
    gate = jnp.concatenate([t[:, 2 * s : 2 * s + w] for s, w in chunks(ff)], axis=1)
    up = jnp.concatenate([t[:, 2 * s + w : 2 * (s + w)] for s, w in chunks(ff)], axis=1)
    return gate, up


def scale_of(wide):
    return lax.rsqrt(jnp.mean(wide * wide, -1, keepdims=True) + EPS)


def sigmoid(t):
    return 0.5 * jnp.tanh(0.5 * t) + 0.5


MESH = pl.DeviceIdType.MESH
Z = 4


def place():
    dp = lax.axis_index("dp")
    return lax.axis_index("rep"), dp // 2, dp % 2


def remote(src, dst, send, recv, rep, z, core):
    return pltpu.make_async_remote_copy(src_ref=src, dst_ref=dst, send_sem=send, recv_sem=recv, device_id=(rep, 2 * z + core), device_id_type=MESH)


def meet(peers):
    barrier = pltpu.get_barrier_semaphore()
    for rep, z, core in peers:
        pl.semaphore_signal(barrier, inc=1, device_id=(rep, 2 * z + core), device_id_type=MESH)
    pl.semaphore_wait(barrier, len(peers))


def z_peers():
    rep, z, core = place()
    return [(rep, (z + i) % Z, core) for i in range(1, Z)]


def rep_peers():
    rep, z, core = place()
    return [((rep + i) % 4, z, core) for i in range(1, 4)]


def sibling():
    rep, z, core = place()
    return rep, z, 1 - core


class Gather:
    SEMS = 3 + 9 + 13

    def __init__(self, gate, up, down, w1, w2, shard, sems):
        self.gate, self.up, self.down, self.w1, self.w2, self.shard, self.sems = gate, up, down, w1, w2, shard, sems
        self.local_sems, self.send_sems, self.recv_sems = sems
        self.r1, self.r2 = gate.shape[1], down.shape[1]
        self.cols = w2.shape[1] // 4

    def block(self, z, core):
        s = 2 * z + core
        return (
            self.w1.at[pl.ds(pl.multiple_of(s * self.r1, self.r1), self.r1), :],
            self.w2.at[pl.ds(pl.multiple_of(s * self.r2, self.r2), self.r2), :],
        )

    def quarter(self, z, core, q):
        s, n = 2 * z + core, self.r1 // 4
        return (
            self.w1.at[pl.ds(pl.multiple_of(s * self.r1 + q * n, n), n), :],
            self.w2.at[pl.ds(pl.multiple_of(s * self.r2, self.r2), self.r2), pl.ds(pl.multiple_of(q * self.cols, self.cols), self.cols)],
        )

    def copies(self, number, srcs, dsts, to):
        return [remote(s, d, self.send_sems.at[2 * number + i], self.recv_sems.at[2 * number + i], *to) for i, (s, d) in enumerate(zip(srcs, dsts))]

    def along_z(self, i):
        rep, z, core = place()
        n = self.r1 // 4
        own = (self.shard.at[pl.ds(pl.multiple_of(rep * n, n), n), :], self.down.at[0, :, pl.ds(pl.multiple_of(rep * self.cols, self.cols), self.cols)])
        return self.copies(i - 1, own, self.quarter(z, core, rep), (rep, (z + i) % Z, core))

    def across(self, i, j):
        rep, z, core = place()
        part = self.quarter((z + Z - i) % Z, core, rep)
        return self.copies(3 + 3 * (i - 1) + j - 1, part, part, ((rep + j) % 4, z, core))

    def inside(self, i, j):
        rep, z, core = place()
        part = self.quarter((z + Z - i) % Z, core, (rep + 4 - j) % 4)
        return self.copies(13 + 4 * (i - 1) + j, part, part, sibling())

    def inside_own(self):
        _, z, core = place()
        return self.copies(12, (self.shard, self.down.at[0]), self.block(z, core), sibling())

    def keep_own(self):
        _, z, core = place()
        return [pltpu.make_async_copy(s, d, self.local_sems.at[i]) for i, (s, d) in enumerate(zip((self.shard, self.down.at[0]), self.block(z, core)))]

    def join(self):
        for s, w in chunks(self.gate.shape[2]):
            self.shard[:, 2 * s : 2 * s + w] = self.gate[0, :, s : s + w]
            self.shard[:, 2 * s + w : 2 * (s + w)] = self.up[0, :, s : s + w]

    def begin(self):
        meet(z_peers() + rep_peers() + [sibling()])
        for i in (2, 1, 3):
            for c in self.along_z(i):
                c.start()
        for c in self.inside_own() + self.keep_own():
            c.start()

    def hand_on(self, i):
        for c in self.along_z(i):
            c.wait_recv()
        for j in range(1, 4):
            for c in self.across(i, j):
                c.start()
        for c in self.inside(i, 0):
            c.start()

    def pass_in(self, i):
        for j in range(1, 4):
            for c in self.across(i, j):
                c.wait_recv()
            for c in self.inside(i, j):
                c.start()

    def end(self):
        for c in self.inside_own():
            c.wait()
        for i in range(1, Z):
            for c in self.along_z(i):
                c.wait_send()
            for j in range(1, 4):
                for c in self.across(i, j):
                    c.wait_send()
            for j in range(4):
                for c in self.inside(i, j):
                    c.wait()
        for c in self.keep_own():
            c.wait()

    @staticmethod
    def scratch(rows_1, width):
        return [
            pltpu.VMEM((rows_1, width), BF), pltpu.SemaphoreType.DMA((2,)),
            pltpu.SemaphoreType.DMA((2 * Gather.SEMS,)), pltpu.SemaphoreType.DMA((2 * Gather.SEMS,)),
        ]


class Scatter:
    def __init__(self, term, own, came, sums, others, load_sems, pair_sems, z_sems):
        self.term, self.own, self.came, self.sums, self.others = term, own, came, sums, others
        self.load_sems, self.pair_sems, self.z_sems = load_sems, pair_sems, z_sems
        self.n = own.shape[1]

    @staticmethod
    def scratch(shape):
        n = shape[0] // 8
        blocks = lambda k: pltpu.VMEM((k, n, shape[1]), BF)
        return [blocks(Z), blocks(Z), blocks(Z), blocks(Z - 1), pltpu.SemaphoreType.DMA((Z,)), pltpu.SemaphoreType.DMA((2, Z)), pltpu.SemaphoreType.DMA((2, Z - 1))]

    SCRATCH = 7

    def block(self, z, core):
        return self.term.at[pl.ds(pl.multiple_of((2 * z + core) * self.n, self.n), self.n), :]

    def pair(self):
        _, _, core = place()
        return [remote(self.block(t, 1 - core), self.came.at[t], self.pair_sems.at[0, t], self.pair_sems.at[1, t], *sibling()) for t in range(Z)]

    def loads(self):
        _, _, core = place()
        return [pltpu.make_async_copy(self.block(t, core), self.own.at[t], self.load_sems.at[t]) for t in range(Z)]

    def along_z(self):
        rep, z, core = place()
        return [remote(self.sums.at[(z + i) % Z], self.others.at[i - 1], self.z_sems.at[0, i - 1], self.z_sems.at[1, i - 1], rep, (z + i) % Z, core) for i in (2, 1, 3)]

    def begin(self):
        meet(z_peers() + [sibling()])
        for c in self.pair() + self.loads():
            c.start()

    def add_pair(self):
        for c in self.pair() + self.loads():
            c.wait()
        for t in range(Z):
            self.sums[t] = (self.own[t].astype(F32) + self.came[t].astype(F32)).astype(BF)

    def send(self):
        for c in self.along_z():
            c.start()

    def end(self, out):
        _, z, _ = place()
        for c in self.along_z():
            c.wait()
        total = self.sums[z].astype(F32)
        for i in range(Z - 1):
            total += self.others[i].astype(F32)
        out[...] = total.astype(BF)

    def run(self, out):
        step, last = pl.program_id(0), pl.num_programs(0) - 1
        pl.when(step == 0)(self.begin)
        pl.when(step == 1)(self.add_pair)
        pl.when(step == 2)(self.send)
        pl.when(step == last)(functools.partial(self.end, out))


def gather_kernel(gate_ref, up_ref, down_ref, w1_ref, w2_ref, *scratch):
    g = Gather(gate_ref, up_ref, down_ref, w1_ref, w2_ref, scratch[0], scratch[1:])
    g.join()
    g.begin()
    for i in (1, 3, 2):
        g.hand_on(i)
    for i in (1, 3, 2):
        g.pass_in(i)
    g.end()


def forward_kernel(h_ref, w1_ref, w2_ref, gate_ref, up_ref, down_ref, o_ref, next_w1_ref, next_w2_ref, p_ref, *scratch):
    g = Gather(gate_ref, up_ref, down_ref, next_w1_ref, next_w2_ref, scratch[0], scratch[1:])
    step = pl.program_id(0)
    pl.when(step == 0)(g.join)
    pl.when(step == 0)(g.begin)
    for at, i in ((2, 1), (3, 3), (4, 2)):
        pl.when(step == at)(functools.partial(g.hand_on, i))
    for at, i in ((5, 1), (6, 3), (7, 2)):
        pl.when(step == at)(functools.partial(g.pass_in, i))
    ff = w2_ref.shape[0]
    wide = h_ref[...].astype(F32)
    a = (wide * scale_of(wide)).astype(BF)
    for s, w in chunks(ff):
        gu = dot(a, w1_ref[:, 2 * s : 2 * (s + w)])
        gate, up = gu[:, :w], gu[:, w:]
        p_ref[:, s : s + w] = (gate * sigmoid(gate) * up).astype(BF)
    o_ref[...] = h_ref[...] + dot(p_ref[...], w2_ref[...]).astype(BF)
    pl.when(step == pl.num_programs(0) - 1)(g.end)


def with_scatter(kernel, inputs, outputs):
    def both(*refs):
        ins, term, rest = refs[:inputs], refs[inputs], refs[inputs + 1 :]
        outs, block, rest = rest[:outputs], rest[outputs], rest[outputs + 1 :]
        own, scratch = rest[: len(rest) - Scatter.SCRATCH], rest[len(rest) - Scatter.SCRATCH :]
        job = Scatter(term, *scratch)
        step, last = pl.program_id(0), pl.num_programs(0) - 1
        pl.when(step == 0)(job.begin)
        pl.when(step == 1)(job.add_pair)
        pl.when(step == 2)(job.send)
        kernel(*ins, *outs, *own)
        pl.when(step == last)(lambda: job.end(block))

    return both


def hidden_kernel(h_ref, by_ref, w1_ref, w2_ref, dgu_ref, at_ref, dw2_ref, p_ref, acc_ref):
    ff = w2_ref.shape[0]
    step = pl.program_id(0)
    wide = h_ref[...].astype(F32)
    a = (wide * scale_of(wide)).astype(BF)
    at_ref[...] = a.T
    by = by_ref[...]
    for s, w in chunks(ff):
        gu = dot(a, w1_ref[:, 2 * s : 2 * (s + w)])
        dp = dot_nt(by, w2_ref[s : s + w, :]).astype(BF).astype(F32)
        gate, up = gu[:, :w], gu[:, w:]
        sg = sigmoid(gate)
        silu = gate * sg
        p_ref[:, s : s + w] = (silu * up).astype(BF)
        dgu_ref[:, 2 * s : 2 * s + w] = (dp * up * (sg + silu * (1 - sg))).astype(BF)
        dgu_ref[:, 2 * s + w : 2 * (s + w)] = (dp * silu).astype(BF)
    term = dot(by.T, p_ref[...])

    @pl.when(step == 0)
    def _():
        acc_ref[...] = term

    @pl.when(step > 0)
    def _():
        acc_ref[...] += term

    @pl.when(step == pl.num_programs(0) - 1)
    def _():
        dw2_ref[...] = acc_ref[...].astype(BF).T


def weights_kernel(at_ref, dgu_ref, dw1_ref):
    dw1_ref[...] = dot(at_ref[...], dgu_ref[...]).astype(BF)


def input_kernel(h_ref, by_ref, dgu_ref, w1_ref, o_ref):
    da = dot_nt(dgu_ref[...], w1_ref[...]).astype(BF).astype(F32)
    wide = h_ref[...].astype(F32)
    scale = scale_of(wide)
    inner = jnp.mean(da * wide, -1, keepdims=True)
    o_ref[...] = by_ref[...] + (scale * da - (scale * scale * scale * inner) * wide).astype(BF)


def params(number=None):
    more = {} if number is None else {"collective_id": number, "has_side_effects": True}
    return pltpu.CompilerParams(dimension_semantics=("arbitrary",), vmem_limit_bytes=VMEM_LIMIT, **more)


def cost(flops, nbytes):
    return pl.CostEstimate(flops=flops, bytes_accessed=nbytes, transcendentals=0)


def whole(shape):
    return pl.BlockSpec(shape, lambda i: (0,) * len(shape))


def rows(width):
    return pl.BlockSpec((TM, width), lambda i: (i, 0))


def of_layer(t, n):
    return pl.BlockSpec((1, *t.shape[1:]), lambda i: (n, 0, 0))


ANY = pl.BlockSpec(memory_space=pl.ANY)


def shapes(*all_of):
    return [jax.ShapeDtypeStruct(s, BF) for s in all_of]


def gather(blocks, n, number):
    (_, r1, ff), (_, r2, d) = blocks[0].shape, blocks[2].shape
    return pl.pallas_call(
        gather_kernel, grid=(1,), name="gather",
        in_specs=[of_layer(t, n) for t in blocks], out_specs=[ANY, ANY],
        out_shape=shapes((8 * r1, 2 * ff), (8 * r2, d)),
        scratch_shapes=Gather.scratch(r1, 2 * ff), compiler_params=params(number), cost_estimate=cost(10**9, 10**6),
    )(*blocks)


def forward(h, w1, w2, blocks, n, number):
    t, d = h.shape
    ff = w2.shape[0]
    return pl.pallas_call(
        forward_kernel, grid=(t // TM,), name="forward",
        in_specs=[rows(d), whole(w1.shape), whole(w2.shape), *(of_layer(b, n) for b in blocks)], out_specs=[rows(d), ANY, ANY],
        out_shape=shapes((t, d), w1.shape, w2.shape),
        scratch_shapes=[pltpu.VMEM((TM, ff), BF), *Gather.scratch(blocks[0].shape[1], 2 * ff)],
        compiler_params=params(number), cost_estimate=cost(6 * t * d * ff, 4 * t * d),
    )(h, w1, w2, *blocks)


def call(kernel, name, grid, in_specs, out_specs, out_shape, scratch, flops, args, term=None, number=None):
    if term is not None:
        kernel = with_scatter(kernel, len(in_specs), len(out_specs))
        block = (term.shape[0] // 8, term.shape[1])
        in_specs, out_specs, args = [*in_specs, ANY], [*out_specs, whole(block)], (*args, term)
        out_shape, scratch = [*out_shape, block], [*scratch, *Scatter.scratch(term.shape)]
    return pl.pallas_call(
        kernel, grid=grid, name=name, in_specs=in_specs, out_specs=out_specs, out_shape=shapes(*out_shape),
        scratch_shapes=scratch, compiler_params=params(number), cost_estimate=cost(flops, 10**7),
    )(*args)


def hidden(h, by, w1, w2, **more):
    t, d = h.shape
    ff = w2.shape[0]
    return call(
        hidden_kernel, "hidden", (t // TM,), [rows(d), rows(d), whole(w1.shape), whole(w2.shape)],
        [rows(2 * ff), pl.BlockSpec((d, TM), lambda i: (0, i)), whole((ff, d))], [(t, 2 * ff), (d, t), (ff, d)],
        [pltpu.VMEM((TM, ff), BF), pltpu.VMEM((d, ff), F32)], 8 * t * d * ff, (h, by, w1, w2), **more,
    )


def by_weights(at, dgu, **more):
    d, t = at.shape
    n = dgu.shape[1]
    return call(
        weights_kernel, "by_weights", (n // 256,), [whole((d, t)), pl.BlockSpec((t, 256), lambda i: (0, i))],
        [pl.BlockSpec((d, 256), lambda i: (0, i))], [(d, n)], [], 2 * t * d * n, (at, dgu), **more,
    )


def by_input(h, by, dgu, w1, **more):
    t, d = h.shape
    n = dgu.shape[1]
    return call(
        input_kernel, "by_input", (t // TM,), [rows(d), rows(d), rows(n), whole(w1.shape)],
        [rows(d)], [(t, d)], [], 2 * t * d * n, (h, by, dgu, w1), **more,
    )


def solution(mesh):
    def step(x, dy, w_gate, w_up, w_down):
        x, by = x[0], dy[0]
        blocks = (w_gate, w_up, w_down)
        w1, w2 = gather(blocks, 0, 0)
        h, v1, v2 = forward(x, w1, w2, blocks, 1, 1)
        dgu, at, t2 = hidden(h, by, v1, v2)
        t1, g2_1 = by_weights(at, dgu, term=t2, number=2)
        (by,) = by_input(h, by, lax.optimization_barrier((dgu, t1))[0], v1)
        dgu, at, t2, g1_1 = hidden(x, by, w1, w2, term=t1, number=3)
        t1, g2_0 = by_weights(at, dgu, term=t2, number=4)
        by, g1_0 = by_input(x, by, dgu, w1, term=t1, number=5)
        gates, ups = zip(parted(g1_0), parted(g1_1))
        return by[None], jnp.stack(gates), jnp.stack(ups), jnp.stack((g2_0, g2_1))

    spread, by_rows = P(("rep", "dp"), None, None), P(None, "dp", None)
    group = P("rep", "dp", None)
    return jax.shard_map(
        step, mesh=mesh, in_specs=(spread, spread, by_rows, by_rows, by_rows),
        out_specs=(spread, group, group, group), check_vma=False,
    )
```

time: 360 us -> 291 us (0.81)
  the two profiles are of different devices: /device:TPU:0 before, /device:TPU:12 now
where the time goes in v1:
time: 291 us; the launch traced here: 290 us
  Pallas kernels  278 us (96%)
  local copies, waits for them, and re-layouts  9.18 us (3%)
    pallas_call x6, Pallas kernels, call(): pl.pallas_call(kernel, grid=grid, name=name, in_specs=in_specs, out_specs...  204 us
    pallas_call x1, Pallas kernels, forward(): pl.pallas_call(forward_kernel, grid=(t // TM,), name='forward', in_specs=...  41.7 us
    pallas_call x1, Pallas kernels, gather(): pl.pallas_call(gather_kernel, grid=(1,), name='gather', in_specs=[of_laye...  32.3 us
    unnamed x17, local copies, waits for them, and re-layouts  8.42 us

profile of v1, /device:TPU:12, one launch (start us, length us, event | category | flops | bytes accessed | tf_op | source)
XLA Modules:
  0.0 289.7 jit_solution(15537803086065715063)
XLA Ops:
  0.6 32.3 %gather.1 = (bf16[512,2816]{1,0:T(8,128)(2,1)}, bf16[1408,512]{1,0:T(8,128)(2,1)}) custom-call(bf16[2,64,1408]{2,1,0:T(8,128)(2,1)} %gate_ref.3, bf16[2,64,1408]{2,1,0:T(8,128)(2,1)} %up_ref.3, bf16[2,176,512]{2,1,0:T(8,128)(2,1)} %down_ref.3), custom_call_target="tpu_custom_call" | custom-call | flops 1000000000 | bytes 1000000 | tf_op jit(solution)/shard_map/gather/pallas_call | solution.py:366
  32.9 41.7 %forward.1 = (bf16[4096,512]{1,0:T(8,128)(2,1)}, bf16[512,2816]{1,0:T(8,128)(2,1)}, bf16[1408,512]{1,0:T(8,128)(2,1)}) custom-call(bf16[4096,512]{1,0:T(8,128)(2,1)} %bitcast.18, bf16[512,2816]{1,0:T(8,128)(2,1)} %get-tuple-element.23.w1_ref.refs_2_.refs_3_, bf16[1408,512]{1,0:T(8,128)(2,1)} %get-tuple-element.24.w2_ref.refs_3_, ...), custom_call_target="tpu_custom_call" | custom-call | flops 17716740096 | bytes 8388608 | tf_op jit(solution)/shard_map/forward/pallas_call | solution.py:377
  74.6 35.7 %hidden.2 = (bf16[4096,2816]{1,0:T(8,128)(2,1)}, bf16[512,4096]{1,0:T(8,128)(2,1)}, bf16[1408,512]{1,0:T(8,128)(2,1)}) custom-call(bf16[4096,512]{1,0:T(8,128)(2,1)} %get-tuple-element.25.h_ref, bf16[4096,512]{1,0:T(8,128)(2,1)} %bitcast.16, bf16[512,2816]{1,0:T(8,128)(2,1)} %get-tuple-element.26.w1_ref, bf16[1408,512]{1,0:T(8,128)(2,1)} %get-tuple-element.27.w2_ref), custom_call_target="tpu_custom_call" | custom-call | flops 23622320128 | bytes 10000000 | tf_op jit(solution)/shard_map/hidden/pallas_call | solution.py:392
  110.3 29.9 %by_weights.2 = (bf16[512,2816]{1,0:T(8,128)(2,1)}, bf16[176,512]{1,0:T(8,128)(2,1)}) custom-call(bf16[512,4096]{1,0:T(8,128)(2,1)} %get-tuple-element.29.refs_0_, bf16[4096,2816]{1,0:T(8,128)(2,1)} %get-tuple-element.32.refs_1_.dgu_ref, bf16[1408,512]{1,0:T(8,128)(2,1)} %get-tuple-element.30.refs_2_), custom_call_target="tpu_custom_call" | custom-call | flops 11811160064 | bytes 10000000 | tf_op jit(solution)/shard_map/by_weights/pallas_call | solution.py:392
  140.2 20.7 %by_input.2.refs_1_ = bf16[4096,512]{1,0:T(8,128)(2,1)} custom-call(bf16[4096,512]{1,0:T(8,128)(2,1)} %get-tuple-element.25.h_ref, bf16[4096,512]{1,0:T(8,128)(2,1)} %bitcast.17, bf16[4096,2816]{1,0:T(8,128)(2,1)} %get-tuple-element.32.refs_1_.dgu_ref, bf16[512,2816]{1,0:T(8,128)(2,1)} %get-tuple-element.26.w1_ref), custom_call_target="tpu_custom_call" | custom-call | flops 11811160064 | bytes 10000000 | tf_op jit(solution)/shard_map/by_input/pallas_call | solution.py:392
  160.9 47.3 %hidden.3 = (bf16[4096,2816]{1,0:T(8,128)(2,1)}, bf16[512,4096]{1,0:T(8,128)(2,1)}, bf16[1408,512]{1,0:T(8,128)(2,1)}, bf16[64,2816]{1,0:T(8,128)(2,1)}) custom-call(bf16[4096,512]{1,0:T(8,128)(2,1)} %bitcast.19, bf16[4096,512]{1,0:T(8,128)(2,1)} %by_input.2.refs_1_, bf16[512,2816]{1,0:T(8,128)(2,1)} %get-tuple-element.23.w1_ref.refs_2_.refs_3_, ...), custom_call_target="tpu_custom_call" | custom-call | flops 23622320128 | bytes 10000000 | tf_op jit(solution)/shard_map/hidden/pallas_call | solution.py:392
  208.3 26.2 %by_weights.3 = (bf16[512,2816]{1,0:T(8,128)(2,1)}, bf16[176,512]{1,0:T(8,128)(2,1)}) custom-call(bf16[512,4096]{1,0:T(8,128)(2,1)} %get-tuple-element.34.refs_0_, bf16[4096,2816]{1,0:T(8,128)(2,1)} %get-tuple-element.33.refs_1_.refs_2_, bf16[1408,512]{1,0:T(8,128)(2,1)} %get-tuple-element.35.refs_2_), custom_call_target="tpu_custom_call" | custom-call | flops 11811160064 | bytes 10000000 | tf_op jit(solution)/shard_map/by_weights/pallas_call | solution.py:392
  234.5 0.0 copy-start.1
  234.5 0.0 copy-start.2
  234.5 0.0 copy-start
  234.5 44.2 %by_input.3 = (bf16[4096,512]{1,0:T(8,128)(2,1)}, bf16[64,2816]{1,0:T(8,128)(2,1)}) custom-call(bf16[4096,512]{1,0:T(8,128)(2,1)} %bitcast.20, bf16[4096,512]{1,0:T(8,128)(2,1)} %by_input.2.refs_1_, bf16[4096,2816]{1,0:T(8,128)(2,1)} %get-tuple-element.33.refs_1_.refs_2_, bf16[512,2816]{1,0:T(8,128)(2,1)} %get-tuple-element.23.w1_ref.refs_2_.refs_3_, ...), custom_call_target="tpu_custom_call" | custom-call | flops 11811160064 | bytes 10000000 | tf_op jit(solution)/shard_map/by_input/pallas_call | solution.py:392
  278.8 0.0 copy-done.1
  278.8 0.0 copy-done.2
  278.8 0.8 pad_maximum_fusion.2
  279.6 0.8 constant_dynamic-update-slice_fusion.17
  280.4 0.8 constant_dynamic-update-slice_fusion.16
  281.1 0.8 constant_dynamic-update-slice_fusion.15
  281.9 0.8 constant_dynamic-update-slice_fusion.14
  282.7 0.8 constant_dynamic-update-slice_fusion.13
  283.5 0.7 constant_dynamic-update-slice_fusion.12
  284.2 0.0 copy-done
  284.3 0.9 pad_maximum_fusion
  285.3 4.5 %copy.30 = bf16[1,4096,512]{2,1,0:T(8,128)(2,1)} copy(bf16[1,4096,512]{2,1,0:T(8,128)(2,1)} %bitcast.9) | data formatting | bytes 8388608
  (6 shorter events, 0.1 us)
Async XLA Ops:
  234.5 44.3 %copy-start.1 = (bf16[176,512]{1,0:T(8,128)(2,1)S(1)}, bf16[176,512]{1,0:T(8,128)(2,1)}, u32[]{:S(2)}) copy-start(bf16[176,512]{1,0:T(8,128)(2,1)} %get-tuple-element.41) | copy-start | bytes 540676
  234.5 44.3 %copy-start.2 = (bf16[176,512]{1,0:T(8,128)(2,1)S(1)}, bf16[176,512]{1,0:T(8,128)(2,1)}, u32[]{:S(2)}) copy-start(bf16[176,512]{1,0:T(8,128)(2,1)} %get-tuple-element.40) | copy-start | bytes 540676
  234.5 49.7 %copy-start = (bf16[64,2816]{1,0:T(8,128)(2,1)S(1)}, bf16[64,2816]{1,0:T(8,128)(2,1)}, u32[]{:S(2)}) copy-start(bf16[64,2816]{1,0:T(8,128)(2,1)} %get-tuple-element.39) | copy-start | bytes 1081348

commit v2 on v1

--- a/solution.py
+++ b/solution.py
@@ -24,17 +24,6 @@
 
 def chunks(ff):
     return [(s, min(CH, ff - s)) for s in range(0, ff, CH)]
-
-
-def joined(gate, up):
-    return jnp.concatenate([t[:, s : s + w] for s, w in chunks(gate.shape[1]) for t in (gate, up)], axis=1)
-
-
-def parted(t):
-    ff = t.shape[1] // 2
-    gate = jnp.concatenate([t[:, 2 * s : 2 * s + w] for s, w in chunks(ff)], axis=1)
-    up = jnp.concatenate([t[:, 2 * s + w : 2 * (s + w)] for s, w in chunks(ff)], axis=1)
-    return gate, up
 
 
 def scale_of(wide):
@@ -183,16 +172,20 @@
 
 
 class Scatter:
-    def __init__(self, term, own, came, sums, others, load_sems, pair_sems, z_sems):
-        self.term, self.own, self.came, self.sums, self.others = term, own, came, sums, others
-        self.load_sems, self.pair_sems, self.z_sems = load_sems, pair_sems, z_sems
-        self.n = own.shape[1]
+    def __init__(self, term, came, sums, others, relay, onward, pair_sems, z_sems):
+        self.term, self.came, self.sums, self.others, self.relay, self.onward = term, came, sums, others, relay, onward
+        self.pair_sems, self.z_sems = pair_sems, z_sems
+        self.n = sums.shape[1]
+        rep, z, core = place()
+        self.rep, self.z, self.core = rep, z, core
+        self.is_end = (z == 0) | (z == 3)
+        self.near = 1 + z // 3
+        self.outer, self.inner = 3 * (z // 2), 3 - z
 
     @staticmethod
-    def scratch(shape):
-        n = shape[0] // 8
-        blocks = lambda k: pltpu.VMEM((k, n, shape[1]), BF)
-        return [blocks(Z), blocks(Z), blocks(Z), blocks(Z - 1), pltpu.SemaphoreType.DMA((Z,)), pltpu.SemaphoreType.DMA((2, Z)), pltpu.SemaphoreType.DMA((2, Z - 1))]
+    def scratch(rows_of, width):
+        blocks = lambda k: pltpu.VMEM((k, rows_of, width), BF)
+        return [blocks(Z), blocks(Z), blocks(2), blocks(2), blocks(2), pltpu.SemaphoreType.DMA((2, Z)), pltpu.SemaphoreType.DMA((2, 4))]
 
     SCRATCH = 7
 
@@ -200,56 +193,83 @@
         return self.term.at[pl.ds(pl.multiple_of((2 * z + core) * self.n, self.n), self.n), :]
 
     def pair(self):
-        _, _, core = place()
-        return [remote(self.block(t, 1 - core), self.came.at[t], self.pair_sems.at[0, t], self.pair_sems.at[1, t], *sibling()) for t in range(Z)]
-
-    def loads(self):
-        _, _, core = place()
-        return [pltpu.make_async_copy(self.block(t, core), self.own.at[t], self.load_sems.at[t]) for t in range(Z)]
-
-    def along_z(self):
-        rep, z, core = place()
-        return [remote(self.sums.at[(z + i) % Z], self.others.at[i - 1], self.z_sems.at[0, i - 1], self.z_sems.at[1, i - 1], rep, (z + i) % Z, core) for i in (2, 1, 3)]
+        return [remote(self.block(t, 1 - self.core), self.came.at[t], self.pair_sems.at[0, t], self.pair_sems.at[1, t], *sibling()) for t in range(Z)]
+
+    def copy(self, src, number, z):
+        slot = self.others.at[number] if number < 2 else self.relay.at[number - 2]
+        return remote(src, slot, self.z_sems.at[0, number], self.z_sems.at[1, number], self.rep, z, self.core)
+
+    def ends_copies(self):
+        z, near = self.z, self.near
+        return [self.copy(self.sums.at[t], number, near) for number, t in ((2, 3 - z), (3, 3 - near), (0, near))]
+
+    def direct(self):
+        return self.copy(self.sums.at[self.outer], 0, self.outer)
+
+    def onwards(self, i):
+        return self.copy(self.onward.at[i], 1, 3 - self.outer) if i == 0 else self.copy2()
+
+    def copy2(self):
+        return remote(self.onward.at[1], self.others.at[1], self.z_sems.at[0, 2], self.z_sems.at[1, 1], self.rep, self.inner, self.core)
 
     def begin(self):
-        meet(z_peers() + [sibling()])
-        for c in self.pair() + self.loads():
+        for c in self.pair():
             c.start()
 
     def add_pair(self):
-        for c in self.pair() + self.loads():
+        for c in self.pair():
             c.wait()
         for t in range(Z):
-            self.sums[t] = (self.own[t].astype(F32) + self.came[t].astype(F32)).astype(BF)
+            self.sums[t] = (self.block(t, self.core)[...].astype(F32) + self.came[t].astype(F32)).astype(BF)
 
     def send(self):
-        for c in self.along_z():
-            c.start()
-
-    def end(self, out):
-        _, z, _ = place()
-        for c in self.along_z():
-            c.wait()
-        total = self.sums[z].astype(F32)
-        for i in range(Z - 1):
-            total += self.others[i].astype(F32)
-        out[...] = total.astype(BF)
-
-    def run(self, out):
-        step, last = pl.program_id(0), pl.num_programs(0) - 1
-        pl.when(step == 0)(self.begin)
-        pl.when(step == 1)(self.add_pair)
-        pl.when(step == 2)(self.send)
-        pl.when(step == last)(functools.partial(self.end, out))
+        @pl.when(self.is_end)
+        def _():
+            for c in self.ends_copies():
+                c.start()
+
+        @pl.when(jnp.logical_not(self.is_end))
+        def _():
+            self.direct().start()
+
+    def add_relay(self, i):
+        @pl.when(jnp.logical_not(self.is_end))
+        def _():
+            self.copy(self.onward.at[i], 2 + i, self.near).wait_recv()
+            to = 3 - self.outer if i == 0 else self.inner
+            self.onward[i] = (self.sums[to].astype(F32) + self.relay[i].astype(F32)).astype(BF)
+
+    def send_relay(self, i):
+        @pl.when(jnp.logical_not(self.is_end))
+        def _():
+            self.onwards(i).start()
+
+    def end(self):
+        for i in range(2):
+            self.copy(self.onward.at[i], i, self.near).wait_recv()
+
+        @pl.when(self.is_end)
+        def _():
+            for c in self.ends_copies():
+                c.wait_send()
+
+        @pl.when(jnp.logical_not(self.is_end))
+        def _():
+            self.direct().wait_send()
+            for i in range(2):
+                self.onwards(i).wait_send()
+
+        total = self.sums[self.z].astype(F32) + self.others[0].astype(F32) + self.others[1].astype(F32)
+        return total.astype(BF)
 
 
 def gather_kernel(gate_ref, up_ref, down_ref, w1_ref, w2_ref, *scratch):
     g = Gather(gate_ref, up_ref, down_ref, w1_ref, w2_ref, scratch[0], scratch[1:])
     g.join()
     g.begin()
-    for i in (1, 3, 2):
+    for i in (2, 1, 3):
         g.hand_on(i)
-    for i in (1, 3, 2):
+    for i in (2, 1, 3):
         g.pass_in(i)
     g.end()
 
@@ -259,9 +279,9 @@
     step = pl.program_id(0)
     pl.when(step == 0)(g.join)
     pl.when(step == 0)(g.begin)
-    for at, i in ((2, 1), (3, 3), (4, 2)):
+    for at, i in ((2, 2), (3, 1), (4, 3)):
         pl.when(step == at)(functools.partial(g.hand_on, i))
-    for at, i in ((5, 1), (6, 3), (7, 2)):
+    for at, i in ((5, 2), (7, 1)):
         pl.when(step == at)(functools.partial(g.pass_in, i))
     ff = w2_ref.shape[0]
     wide = h_ref[...].astype(F32)
@@ -271,66 +291,119 @@
         gate, up = gu[:, :w], gu[:, w:]
         p_ref[:, s : s + w] = (gate * sigmoid(gate) * up).astype(BF)
     o_ref[...] = h_ref[...] + dot(p_ref[...], w2_ref[...]).astype(BF)
-    pl.when(step == pl.num_programs(0) - 1)(g.end)
-
-
-def with_scatter(kernel, inputs, outputs):
-    def both(*refs):
-        ins, term, rest = refs[:inputs], refs[inputs], refs[inputs + 1 :]
-        outs, block, rest = rest[:outputs], rest[outputs], rest[outputs + 1 :]
-        own, scratch = rest[: len(rest) - Scatter.SCRATCH], rest[len(rest) - Scatter.SCRATCH :]
-        job = Scatter(term, *scratch)
-        step, last = pl.program_id(0), pl.num_programs(0) - 1
-        pl.when(step == 0)(job.begin)
-        pl.when(step == 1)(job.add_pair)
-        pl.when(step == 2)(job.send)
-        kernel(*ins, *outs, *own)
-        pl.when(step == last)(lambda: job.end(block))
-
-    return both
-
-
-def hidden_kernel(h_ref, by_ref, w1_ref, w2_ref, dgu_ref, at_ref, dw2_ref, p_ref, acc_ref):
+    pl.when(step == pl.num_programs(0) - 1)(lambda: (g.pass_in(3), g.end()) and None)
+
+
+def backward_kernel(tiles, h_ref, by_ref, w1_ref, w2_ref, o_ref, dgate_ref, dup_ref, ddown_ref, dgu_ref, at_ref, p_ref, acc_ref, dw1_ref, dw2_ref, *scratch):
     ff = w2_ref.shape[0]
+    parts = halves(ff)
+    runs = [[c for c in chunks(ff) if lo <= c[0] < hi] for lo, hi in parts]
+    s1, s2, s3, s4, count = marks(tiles, ff)
     step = pl.program_id(0)
-    wide = h_ref[...].astype(F32)
-    a = (wide * scale_of(wide)).astype(BF)
-    at_ref[...] = a.T
-    by = by_ref[...]
-    for s, w in chunks(ff):
-        gu = dot(a, w1_ref[:, 2 * s : 2 * (s + w)])
-        dp = dot_nt(by, w2_ref[s : s + w, :]).astype(BF).astype(F32)
-        gate, up = gu[:, :w], gu[:, w:]
-        sg = sigmoid(gate)
-        silu = gate * sg
-        p_ref[:, s : s + w] = (silu * up).astype(BF)
-        dgu_ref[:, 2 * s : 2 * s + w] = (dp * up * (sg + silu * (1 - sg))).astype(BF)
-        dgu_ref[:, 2 * s + w : 2 * (s + w)] = (dp * silu).astype(BF)
-    term = dot(by.T, p_ref[...])
-
-    @pl.when(step == 0)
+    n = Scatter.SCRATCH
+    first, second = (
+        Scatter(dw1_ref.at[:, 2 * lo : 2 * hi], *scratch[n * k : n * (k + 1)]) for k, (lo, hi) in enumerate(parts)
+    )
+    down = Scatter(dw2_ref, *scratch[2 * n :])
+    before = [
+        (s2, first.begin), (s2 + 1, first.add_pair), (s2 + 4, lambda: first.add_relay(0)), (s2 + 6, lambda: first.add_relay(1)),
+        (s3, down.begin), (s3 + 2, down.add_pair), (s4 + 1, lambda: down.add_relay(0)), (s4 + 3, lambda: down.add_relay(1)),
+        (s4, second.begin), (s4 + 1, second.add_pair), (s4 + 6, lambda: second.add_relay(0)),
+    ]
+    after = [
+        (s2 + 1, first.send), (s2 + 4, lambda: first.send_relay(0)), (s2 + 6, lambda: first.send_relay(1)),
+        (s3 + 2, down.send), (s4 + 1, lambda: down.send_relay(0)), (s4 + 3, lambda: down.send_relay(1)),
+        (s4 + 1, second.send), (s4 + 6, lambda: second.send_relay(0)),
+    ]
+
+    def first_end():
+        put(first.end(), runs[0])
+
+    def put(block, of):
+        start = 2 * of[0][0]
+        for s, w in of:
+            at = 2 * s - start
+            dgate_ref[:, s : s + w] = block[:, at : at + w]
+            dup_ref[:, s : s + w] = block[:, at + w : at + 2 * w]
+
+    before.append((s3 + 1, first_end))
+    pl.when(step == 0)(lambda: meet(z_peers() + [sibling()]))
+    for at, do in before:
+        pl.when(step == at)(do)
+
+    def hidden(part, tile):
+        rows_of = pl.ds(pl.multiple_of(tile * TM, TM), TM)
+        wide = h_ref[...].astype(F32)
+        a = (wide * scale_of(wide)).astype(BF)
+        if part == 0:
+            at_ref[:, rows_of] = a.T
+        by = by_ref[...]
+        lo, hi = parts[part]
+        for s, w in runs[part]:
+            gu = dot(a, w1_ref[:, 2 * s : 2 * (s + w)])
+            dp = dot_nt(by, w2_ref[s : s + w, :]).astype(BF).astype(F32)
+            gate, up = gu[:, :w], gu[:, w:]
+            sg = sigmoid(gate)
+            silu = gate * sg
+            p_ref[:, s - lo : s - lo + w] = (silu * up).astype(BF)
+            dgu_ref[rows_of, 2 * s : 2 * s + w] = (dp * up * (sg + silu * (1 - sg))).astype(BF)
+            dgu_ref[rows_of, 2 * s + w : 2 * (s + w)] = (dp * silu).astype(BF)
+        term = dot(by.T, p_ref[:, : hi - lo])
+
+        @pl.when(tile == 0)
+        def _():
+            acc_ref[:, lo:hi] = term
+
+        @pl.when(tile > 0)
+        def _():
+            acc_ref[:, lo:hi] += term
+
+        if part == 1:
+
+            @pl.when(tile == tiles - 1)
+            def _():
+                dw2_ref[...] = acc_ref[...].astype(BF).T
+
+    pl.when(step < s1)(lambda: hidden(0, step))
+    pl.when((step >= s2) & (step < s3))(lambda: hidden(1, step - s2))
+
+    def weights(number):
+        columns = pl.ds(pl.multiple_of(number * 256, 256), 256)
+        dw1_ref[:, columns] = dot(at_ref[...], dgu_ref[:, columns]).astype(BF)
+
+    pl.when(((step >= s1) & (step < s2)) | ((step >= s3) & (step < s4)))(
+        lambda: weights(jnp.where(step < s2, step - s1, step - s3 + s2 - s1))
+    )
+
+    @pl.when(step >= s4)
     def _():
-        acc_ref[...] = term
-
-    @pl.when(step > 0)
+        rows_of = pl.ds(pl.multiple_of((step - s4) * TM, TM), TM)
+        da = dot_nt(dgu_ref[rows_of, :], w1_ref[...]).astype(BF).astype(F32)
+        wide = h_ref[...].astype(F32)
+        scale = scale_of(wide)
+        inner = jnp.mean(da * wide, -1, keepdims=True)
+        o_ref[...] = by_ref[...] + (scale * da - (scale * scale * scale * inner) * wide).astype(BF)
+
+    for at, do in after:
+        pl.when(step == at)(do)
+
+    @pl.when(step == count - 1)
     def _():
-        acc_ref[...] += term
-
-    @pl.when(step == pl.num_programs(0) - 1)
-    def _():
-        dw2_ref[...] = acc_ref[...].astype(BF).T
-
-
-def weights_kernel(at_ref, dgu_ref, dw1_ref):
-    dw1_ref[...] = dot(at_ref[...], dgu_ref[...]).astype(BF)
-
-
-def input_kernel(h_ref, by_ref, dgu_ref, w1_ref, o_ref):
-    da = dot_nt(dgu_ref[...], w1_ref[...]).astype(BF).astype(F32)
-    wide = h_ref[...].astype(F32)
-    scale = scale_of(wide)
-    inner = jnp.mean(da * wide, -1, keepdims=True)
-    o_ref[...] = by_ref[...] + (scale * da - (scale * scale * scale * inner) * wide).astype(BF)
+        second.add_relay(1)
+        ddown_ref[...] = down.end()
+        second.send_relay(1)
+        put(second.end(), runs[1])
+
+
+def halves(ff):
+    cut = chunks(ff)[(len(chunks(ff)) + 1) // 2][0]
+    return (0, cut), (cut, ff)
+
+
+def marks(tiles, ff):
+    (_, cut), _ = halves(ff)
+    a, b = 2 * cut // 256, 2 * (ff - cut) // 256
+    return tiles, tiles + a, 2 * tiles + a, 2 * tiles + a + b, 3 * tiles + a + b
 
 
 def params(number=None):
@@ -383,44 +456,33 @@
     )(h, w1, w2, *blocks)
 
 
-def call(kernel, name, grid, in_specs, out_specs, out_shape, scratch, flops, args, term=None, number=None):
-    if term is not None:
-        kernel = with_scatter(kernel, len(in_specs), len(out_specs))
-        block = (term.shape[0] // 8, term.shape[1])
-        in_specs, out_specs, args = [*in_specs, ANY], [*out_specs, whole(block)], (*args, term)
-        out_shape, scratch = [*out_shape, block], [*scratch, *Scatter.scratch(term.shape)]
-    return pl.pallas_call(
-        kernel, grid=grid, name=name, in_specs=in_specs, out_specs=out_specs, out_shape=shapes(*out_shape),
-        scratch_shapes=scratch, compiler_params=params(number), cost_estimate=cost(flops, 10**7),
-    )(*args)
-
-
-def hidden(h, by, w1, w2, **more):
+def once(shape):
+    return pl.BlockSpec(shape, lambda i: (0,) * len(shape), pipeline_mode=pl.Buffered(buffer_count=1))
+
+
+def backward(h, by, w1, w2, number):
     t, d = h.shape
     ff = w2.shape[0]
-    return call(
-        hidden_kernel, "hidden", (t // TM,), [rows(d), rows(d), whole(w1.shape), whole(w2.shape)],
-        [rows(2 * ff), pl.BlockSpec((d, TM), lambda i: (0, i)), whole((ff, d))], [(t, 2 * ff), (d, t), (ff, d)],
-        [pltpu.VMEM((TM, ff), BF), pltpu.VMEM((d, ff), F32)], 8 * t * d * ff, (h, by, w1, w2), **more,
-    )
-
-
-def by_weights(at, dgu, **more):
-    d, t = at.shape
-    n = dgu.shape[1]
-    return call(
-        weights_kernel, "by_weights", (n // 256,), [whole((d, t)), pl.BlockSpec((t, 256), lambda i: (0, i))],
-        [pl.BlockSpec((d, 256), lambda i: (0, i))], [(d, n)], [], 2 * t * d * n, (at, dgu), **more,
-    )
-
-
-def by_input(h, by, dgu, w1, **more):
-    t, d = h.shape
-    n = dgu.shape[1]
-    return call(
-        input_kernel, "by_input", (t // TM,), [rows(d), rows(d), rows(n), whole(w1.shape)],
-        [rows(d)], [(t, d)], [], 2 * t * d * n, (h, by, dgu, w1), **more,
-    )
+    tiles = t // TM
+    s1, s2, s3, s4, count = marks(tiles, ff)
+
+    def tile(i):
+        return jnp.where(i < s1, i, jnp.where(i < s2, 0, jnp.where(i < s3, i - s2, jnp.where(i < s4, 0, i - s4)))), 0
+
+    r1, r2 = d // 8, ff // 8
+    (_, cut), _ = halves(ff)
+    return pl.pallas_call(
+        functools.partial(backward_kernel, tiles), grid=(count,), name="backward",
+        in_specs=[pl.BlockSpec((TM, d), tile), pl.BlockSpec((TM, d), tile), once(w1.shape), once(w2.shape)],
+        out_specs=[pl.BlockSpec((TM, d), lambda i: (jnp.maximum(i - s4, 0), 0)), whole((r1, ff)), whole((r1, ff)), whole((r2, d))],
+        out_shape=shapes((t, d), (r1, ff), (r1, ff), (r2, d)),
+        scratch_shapes=[
+            pltpu.VMEM((t, 2 * ff), BF), pltpu.VMEM((d, t), BF), pltpu.VMEM((TM, cut), BF), pltpu.VMEM((d, ff), F32),
+            pltpu.VMEM((d, 2 * ff), BF), pltpu.VMEM((ff, d), BF),
+            *Scatter.scratch(r1, 2 * cut), *Scatter.scratch(r1, 2 * (ff - cut)), *Scatter.scratch(r2, d),
+        ],
+        compiler_params=params(number), cost_estimate=cost(16 * t * d * ff, 10**7),
+    )(h, by, w1, w2)
 
 
 def solution(mesh):
@@ -429,14 +491,9 @@
         blocks = (w_gate, w_up, w_down)
         w1, w2 = gather(blocks, 0, 0)
         h, v1, v2 = forward(x, w1, w2, blocks, 1, 1)
-        dgu, at, t2 = hidden(h, by, v1, v2)
-        t1, g2_1 = by_weights(at, dgu, term=t2, number=2)
-        (by,) = by_input(h, by, lax.optimization_barrier((dgu, t1))[0], v1)
-        dgu, at, t2, g1_1 = hidden(x, by, w1, w2, term=t1, number=3)
-        t1, g2_0 = by_weights(at, dgu, term=t2, number=4)
-        by, g1_0 = by_input(x, by, dgu, w1, term=t1, number=5)
-        gates, ups = zip(parted(g1_0), parted(g1_1))
-        return by[None], jnp.stack(gates), jnp.stack(ups), jnp.stack((g2_0, g2_1))
+        by, *last = backward(h, by, v1, v2, 2)
+        by, *first = backward(x, by, w1, w2, 3)
+        return (by[None], *(jnp.stack(pair) for pair in zip(first, last)))
 
     spread, by_rows = P(("rep", "dp"), None, None), P(None, "dp", None)
     group = P("rep", "dp", None)

time: 291 us -> 260 us (0.89)
  the two profiles are of different devices: /device:TPU:12 before, /device:TPU:0 now
where the time goes in v2:
time: 260 us
  Pallas kernels  251 us (97%)
  local copies, waits for them, and re-layouts  4.48 us (2%)
  other arithmetic  3.63 us (1%)
    pallas_call x2, Pallas kernels, backward(): pl.pallas_call(functools.partial(backward_kernel, tiles), grid=(count,),...  176 us
    pallas_call x1, Pallas kernels, forward(): pl.pallas_call(forward_kernel, grid=(t // TM,), name='forward', in_specs=...  37.4 us
    pallas_call x1, Pallas kernels, gather(): pl.pallas_call(gather_kernel, grid=(1,), name='gather', in_specs=[of_laye...  37.1 us

profile of v2, /device:TPU:0, one launch (start us, length us, event | category | flops | bytes accessed | tf_op | source)
XLA Modules:
  0.0 259.7 jit_solution(12644957843508157530)
XLA Ops:
  0.6 37.1 %gather.1 = (bf16[512,2816]{1,0:T(8,128)(2,1)}, bf16[1408,512]{1,0:T(8,128)(2,1)}) custom-call(bf16[2,64,1408]{2,1,0:T(8,128)(2,1)} %gate_ref.3, bf16[2,64,1408]{2,1,0:T(8,128)(2,1)} %up_ref.3, bf16[2,176,512]{2,1,0:T(8,128)(2,1)} %down_ref.3), custom_call_target="tpu_custom_call" | custom-call | flops 1000000000 | bytes 1000000 | tf_op jit(solution)/shard_map/gather/pallas_call | solution.py:439
  37.8 37.4 %forward.1 = (bf16[4096,512]{1,0:T(8,128)(2,1)}, bf16[512,2816]{1,0:T(8,128)(2,1)}, bf16[1408,512]{1,0:T(8,128)(2,1)}) custom-call(bf16[4096,512]{1,0:T(8,128)(2,1)} %bitcast.17, bf16[512,2816]{1,0:T(8,128)(2,1)} %get-tuple-element.17.w1_ref, bf16[1408,512]{1,0:T(8,128)(2,1)} %get-tuple-element.18.w2_ref, bf16[2,64,1408]{2,1,0:T(8,128)(2,1)} %gate_ref.3, ...), custom_call_target="tpu_custom_call" | custom-call | flops 17716740096 | bytes 8388608 | tf_op jit(solution)/shard_map/forward/pallas_call | solution.py:450
  75.1 87.1 %backward.2 = (bf16[4096,512]{1,0:T(8,128)(2,1)}, bf16[64,1408]{1,0:T(8,128)(2,1)}, bf16[64,1408]{1,0:T(8,128)(2,1)}, bf16[176,512]{1,0:T(8,128)(2,1)}) custom-call(bf16[4096,512]{1,0:T(8,128)(2,1)} %get-tuple-element.19.h_ref, bf16[4096,512]{1,0:T(8,128)(2,1)} %bitcast.16, bf16[512,2816]{1,0:T(8,128)(2,1)} %get-tuple-element.20.w1_ref, ...), custom_call_target="tpu_custom_call" | custom-call | flops 47244640256 | bytes 10000000 | tf_op jit(solution)/shard_map/backward/pallas_call | solution.py:474
  162.2 0.0 copy-start.1
  162.3 0.0 copy-start.2
  162.3 0.0 copy-start
  162.3 89.3 %backward.3 = (bf16[4096,512]{1,0:T(8,128)(2,1)}, bf16[64,1408]{1,0:T(8,128)(2,1)}, bf16[64,1408]{1,0:T(8,128)(2,1)}, bf16[176,512]{1,0:T(8,128)(2,1)}) custom-call(bf16[4096,512]{1,0:T(8,128)(2,1)} %bitcast.18, bf16[4096,512]{1,0:T(8,128)(2,1)} %get-tuple-element.22.by_ref, bf16[512,2816]{1,0:T(8,128)(2,1)} %get-tuple-element.17.w1_ref, ...), custom_call_target="tpu_custom_call" | custom-call | flops 47244640256 | bytes 10000000 | tf_op jit(solution)/shard_map/backward/pallas_call | solution.py:474
  251.6 0.0 copy-done.1
  251.6 0.0 copy-done.2
  251.6 1.9 pad_maximum_fusion
  253.5 0.0 copy-done
  253.5 1.7 pad_maximum_fusion.2
  255.2 4.5 %copy.10 = bf16[1,4096,512]{2,1,0:T(8,128)(2,1)} copy(bf16[1,4096,512]{2,1,0:T(8,128)(2,1)} %bitcast.9) | data formatting | bytes 8388608
Async XLA Ops:
  162.2 89.3 %copy-start.1 = (bf16[64,1408]{1,0:T(8,128)(2,1)S(1)}, bf16[64,1408]{1,0:T(8,128)(2,1)}, u32[]{:S(2)}) copy-start(bf16[64,1408]{1,0:T(8,128)(2,1)} %get-tuple-element.25) | copy-start | bytes 540676
  162.3 89.3 %copy-start.2 = (bf16[64,1408]{1,0:T(8,128)(2,1)S(1)}, bf16[64,1408]{1,0:T(8,128)(2,1)}, u32[]{:S(2)}) copy-start(bf16[64,1408]{1,0:T(8,128)(2,1)} %get-tuple-element.27) | copy-start | bytes 540676
  162.3 91.3 %copy-start = (bf16[176,512]{1,0:T(8,128)(2,1)S(1)}, bf16[176,512]{1,0:T(8,128)(2,1)}, u32[]{:S(2)}) copy-start(bf16[176,512]{1,0:T(8,128)(2,1)} %get-tuple-element.29) | copy-start | bytes 540676

commit v3 on v2

--- a/solution.py
+++ b/solution.py
@@ -1,3 +1,4 @@
+import copy
 import functools
 
 import jax
@@ -77,6 +78,12 @@
         self.local_sems, self.send_sems, self.recv_sems = sems
         self.r1, self.r2 = gate.shape[1], down.shape[1]
         self.cols = w2.shape[1] // 4
+        self.which = (0, 1)
+
+    def only(self, *which):
+        part = copy.copy(self)
+        part.which = which
+        return part
 
     def block(self, z, core):
         s = 2 * z + core
@@ -93,7 +100,7 @@
         )
 
     def copies(self, number, srcs, dsts, to):
-        return [remote(s, d, self.send_sems.at[2 * number + i], self.recv_sems.at[2 * number + i], *to) for i, (s, d) in enumerate(zip(srcs, dsts))]
+        return [remote(srcs[i], dsts[i], self.send_sems.at[2 * number + i], self.recv_sems.at[2 * number + i], *to) for i in self.which]
 
     def along_z(self, i):
         rep, z, core = place()
@@ -117,7 +124,8 @@
 
     def keep_own(self):
         _, z, core = place()
-        return [pltpu.make_async_copy(s, d, self.local_sems.at[i]) for i, (s, d) in enumerate(zip((self.shard, self.down.at[0]), self.block(z, core)))]
+        srcs, dsts = (self.shard, self.down.at[0]), self.block(z, core)
+        return [pltpu.make_async_copy(srcs[i], dsts[i], self.local_sems.at[i]) for i in self.which]
 
     def join(self):
         for s, w in chunks(self.gate.shape[2]):
@@ -125,7 +133,6 @@
             self.shard[:, 2 * s + w : 2 * (s + w)] = self.up[0, :, s : s + w]
 
     def begin(self):
-        meet(z_peers() + rep_peers() + [sibling()])
         for i in (2, 1, 3):
             for c in self.along_z(i):
                 c.start()
@@ -148,9 +155,19 @@
             for c in self.inside(i, j):
                 c.start()
 
-    def end(self):
+    def arrived(self):
         for c in self.inside_own():
+            c.wait_recv()
+        for i in range(1, Z):
+            for j in range(4):
+                for c in self.inside(i, j):
+                    c.wait_recv()
+        for c in self.keep_own():
             c.wait()
+
+    def sent(self):
+        for c in self.inside_own():
+            c.wait_send()
         for i in range(1, Z):
             for c in self.along_z(i):
                 c.wait_send()
@@ -159,9 +176,7 @@
                     c.wait_send()
             for j in range(4):
                 for c in self.inside(i, j):
-                    c.wait()
-        for c in self.keep_own():
-            c.wait()
+                    c.wait_send()
 
     @staticmethod
     def scratch(rows_1, width):
@@ -263,35 +278,71 @@
         return total.astype(BF)
 
 
-def gather_kernel(gate_ref, up_ref, down_ref, w1_ref, w2_ref, *scratch):
-    g = Gather(gate_ref, up_ref, down_ref, w1_ref, w2_ref, scratch[0], scratch[1:])
-    g.join()
-    g.begin()
-    for i in (2, 1, 3):
-        g.hand_on(i)
-    for i in (2, 1, 3):
-        g.pass_in(i)
-    g.end()
-
-
-def forward_kernel(h_ref, w1_ref, w2_ref, gate_ref, up_ref, down_ref, o_ref, next_w1_ref, next_w2_ref, p_ref, *scratch):
-    g = Gather(gate_ref, up_ref, down_ref, next_w1_ref, next_w2_ref, scratch[0], scratch[1:])
+ORDER = (2, 1, 3)
+
+
+def forward_kernel(
+    tiles, h_ref, gates, ups, downs, next_gates, next_ups, next_downs,
+    o_ref, w1_ref, w2_ref, next_w1_ref, next_w2_ref, v1_ref, v2_ref, p_ref, out_sems, *scratch,
+):
+    half = len(scratch) // 2
+    now = Gather(gates, ups, downs, v1_ref, v2_ref, scratch[0], scratch[1:half])
+    later = Gather(next_gates, next_ups, next_downs, next_w1_ref, next_w2_ref, scratch[half], scratch[half + 1 :])
     step = pl.program_id(0)
-    pl.when(step == 0)(g.join)
-    pl.when(step == 0)(g.begin)
-    for at, i in ((2, 2), (3, 1), (4, 3)):
-        pl.when(step == at)(functools.partial(g.hand_on, i))
-    for at, i in ((5, 2), (7, 1)):
-        pl.when(step == at)(functools.partial(g.pass_in, i))
-    ff = w2_ref.shape[0]
-    wide = h_ref[...].astype(F32)
-    a = (wide * scale_of(wide)).astype(BF)
-    for s, w in chunks(ff):
-        gu = dot(a, w1_ref[:, 2 * s : 2 * (s + w)])
-        gate, up = gu[:, :w], gu[:, w:]
-        p_ref[:, s : s + w] = (gate * sigmoid(gate) * up).astype(BF)
-    o_ref[...] = h_ref[...] + dot(p_ref[...], w2_ref[...]).astype(BF)
-    pl.when(step == pl.num_programs(0) - 1)(lambda: (g.pass_in(3), g.end()) and None)
+    w1, w2 = now.only(0), now.only(1)
+    next_w1, next_w2 = later.only(0), later.only(1)
+    out = [pltpu.make_async_copy(v, w, out_sems.at[i]) for i, (v, w) in enumerate(((v1_ref, w1_ref), (v2_ref, w2_ref)))]
+
+    @pl.when(step == 0)
+    def _():
+        now.join()
+        meet(z_peers() + rep_peers() + [sibling()])
+        w1.begin()
+        w2.begin()
+        later.join()
+        for i in ORDER:
+            w1.hand_on(i)
+        next_w1.begin()
+        for i in ORDER:
+            w2.hand_on(i)
+        for i in ORDER:
+            w1.pass_in(i)
+        next_w2.begin()
+        w1.arrived()
+        out[0].start()
+
+    for at, do in (
+        (1, lambda: [w2.pass_in(2), next_w1.hand_on(2)]), (2, lambda: [w2.pass_in(1), next_w1.hand_on(1)]),
+        (3, lambda: [w2.pass_in(3), next_w1.hand_on(3)]), (4, lambda: next_w2.hand_on(2)), (5, lambda: next_w2.hand_on(1)),
+        (6, lambda: next_w2.hand_on(3)), (8, lambda: [w2.arrived(), out[1].start()]), (9, lambda: next_w1.pass_in(2)),
+        (10, lambda: next_w1.pass_in(1)), (11, lambda: next_w1.pass_in(3)), (13, lambda: next_w2.pass_in(2)), (14, lambda: next_w2.pass_in(1)),
+    ):
+        pl.when(step == at)(lambda do=do: do() and None)
+
+    ff = v2_ref.shape[0]
+    rows_of = pl.ds(pl.multiple_of(step % tiles * TM, TM), TM)
+
+    @pl.when(step < tiles)
+    def _():
+        wide = h_ref[...].astype(F32)
+        a = (wide * scale_of(wide)).astype(BF)
+        for s, w in chunks(ff):
+            gu = dot(a, v1_ref[:, 2 * s : 2 * (s + w)])
+            gate, up = gu[:, :w], gu[:, w:]
+            p_ref[rows_of, s : s + w] = (gate * sigmoid(gate) * up).astype(BF)
+
+    @pl.when(step >= tiles)
+    def _():
+        o_ref[...] = h_ref[...] + dot(p_ref[rows_of, :], v2_ref[...]).astype(BF)
+
+    @pl.when(step == 2 * tiles - 1)
+    def _():
+        next_w2.pass_in(3)
+        later.arrived()
+        now.sent()
+        later.sent()
+        for c in out:
+            c.wait()
 
 
 def backward_kernel(tiles, h_ref, by_ref, w1_ref, w2_ref, o_ref, dgate_ref, dup_ref, ddown_ref, dgu_ref, at_ref, p_ref, acc_ref, dw1_ref, dw2_ref, *scratch):
@@ -434,26 +485,22 @@
     return [jax.ShapeDtypeStruct(s, BF) for s in all_of]
 
 
-def gather(blocks, n, number):
-    (_, r1, ff), (_, r2, d) = blocks[0].shape, blocks[2].shape
+def forward(h, blocks, number):
+    t, d = h.shape
+    (_, r1, ff), r2 = blocks[0].shape, blocks[2].shape[1]
+    tiles = t // TM
+    w1, w2 = (8 * r1, 2 * ff), (8 * r2, d)
     return pl.pallas_call(
-        gather_kernel, grid=(1,), name="gather",
-        in_specs=[of_layer(t, n) for t in blocks], out_specs=[ANY, ANY],
-        out_shape=shapes((8 * r1, 2 * ff), (8 * r2, d)),
-        scratch_shapes=Gather.scratch(r1, 2 * ff), compiler_params=params(number), cost_estimate=cost(10**9, 10**6),
-    )(*blocks)
-
-
-def forward(h, w1, w2, blocks, n, number):
-    t, d = h.shape
-    ff = w2.shape[0]
-    return pl.pallas_call(
-        forward_kernel, grid=(t // TM,), name="forward",
-        in_specs=[rows(d), whole(w1.shape), whole(w2.shape), *(of_layer(b, n) for b in blocks)], out_specs=[rows(d), ANY, ANY],
-        out_shape=shapes((t, d), w1.shape, w2.shape),
-        scratch_shapes=[pltpu.VMEM((TM, ff), BF), *Gather.scratch(blocks[0].shape[1], 2 * ff)],
+        functools.partial(forward_kernel, tiles), grid=(2 * tiles,), name="forward",
+        in_specs=[pl.BlockSpec((TM, d), lambda i: (i % tiles, 0)), *(of_layer(b, n) for n in range(2) for b in blocks)],
+        out_specs=[pl.BlockSpec((TM, d), lambda i: (jnp.maximum(i - tiles, 0), 0)), ANY, ANY, ANY, ANY],
+        out_shape=shapes((t, d), w1, w2, w1, w2),
+        scratch_shapes=[
+            pltpu.VMEM(w1, BF), pltpu.VMEM(w2, BF), pltpu.VMEM((t, ff), BF), pltpu.SemaphoreType.DMA((2,)),
+            *Gather.scratch(r1, 2 * ff), *Gather.scratch(r1, 2 * ff),
+        ],
         compiler_params=params(number), cost_estimate=cost(6 * t * d * ff, 4 * t * d),
-    )(h, w1, w2, *blocks)
+    )(h, *blocks, *blocks)
 
 
 def once(shape):
@@ -489,8 +536,7 @@
     def step(x, dy, w_gate, w_up, w_down):
         x, by = x[0], dy[0]
         blocks = (w_gate, w_up, w_down)
-        w1, w2 = gather(blocks, 0, 0)
-        h, v1, v2 = forward(x, w1, w2, blocks, 1, 1)
+        h, w1, w2, v1, v2 = forward(x, blocks, 1)
         by, *last = backward(h, by, v1, v2, 2)
         by, *first = backward(x, by, w1, w2, 3)
         return (by[None], *(jnp.stack(pair) for pair in zip(first, last)))

time: 260 us -> 244 us (0.938)
  Pallas kernels: 251 us -> 235 us
    pallas_call x2 -> x1, Pallas kernels: 74.5 us -> 57.4 us  [forward(): pl.pallas_call(functools.partial(forward_kernel, tiles), grid=(2 * tiles,...]
where the time goes in v3:
time: 244 us
  Pallas kernels  235 us (96%)
  local copies, waits for them, and re-layouts  4.48 us (2%)
  other arithmetic  3.63 us (1%)
    pallas_call x2, Pallas kernels, backward(): pl.pallas_call(functools.partial(backward_kernel, tiles), grid=(count,),...  177 us
    pallas_call x1, Pallas kernels, forward(): pl.pallas_call(functools.partial(forward_kernel, tiles), grid=(2 * tiles,...  57.4 us

profile of v3, /device:TPU:0, one launch (start us, length us, event | category | flops | bytes accessed | tf_op | source)
XLA Modules:
  0.0 243.6 jit_solution(13459788965450130825)
XLA Ops:
  0.6 57.4 %forward.1 = (bf16[4096,512]{1,0:T(8,128)(2,1)}, bf16[512,2816]{1,0:T(8,128)(2,1)}, bf16[1408,512]{1,0:T(8,128)(2,1)}, bf16[512,2816]{1,0:T(8,128)(2,1)}, bf16[1408,512]{1,0:T(8,128)(2,1)}) custom-call(bf16[4096,512]{1,0:T(8,128)(2,1)} %bitcast.17, bf16[2,64,1408]{2,1,0:T(8,128)(2,1)} %next_gates.1, bf16[2,64,1408]{2,1,0:T(8,128)(2,1)} %next_ups.1, ...), custom_call_target="tpu_custom_call" | custom-call | flops 17716740096 | bytes 8388608 | tf_op jit(solution)/shard_map/forward/pallas_call | solution.py:493
  58.0 88.5 %backward.2 = (bf16[4096,512]{1,0:T(8,128)(2,1)}, bf16[64,1408]{1,0:T(8,128)(2,1)}, bf16[64,1408]{1,0:T(8,128)(2,1)}, bf16[176,512]{1,0:T(8,128)(2,1)}) custom-call(bf16[4096,512]{1,0:T(8,128)(2,1)} %get-tuple-element.17.h_ref, bf16[4096,512]{1,0:T(8,128)(2,1)} %bitcast.16, bf16[512,2816]{1,0:T(8,128)(2,1)} %get-tuple-element.18.w1_ref, ...), custom_call_target="tpu_custom_call" | custom-call | flops 47244640256 | bytes 10000000 | tf_op jit(solution)/shard_map/backward/pallas_call | solution.py:521
  146.6 0.0 copy-start.1
  146.6 0.0 copy-start.2
  146.6 0.0 copy-start
  146.6 88.9 %backward.3 = (bf16[4096,512]{1,0:T(8,128)(2,1)}, bf16[64,1408]{1,0:T(8,128)(2,1)}, bf16[64,1408]{1,0:T(8,128)(2,1)}, bf16[176,512]{1,0:T(8,128)(2,1)}) custom-call(bf16[4096,512]{1,0:T(8,128)(2,1)} %bitcast.18, bf16[4096,512]{1,0:T(8,128)(2,1)} %get-tuple-element.20.by_ref, bf16[512,2816]{1,0:T(8,128)(2,1)} %get-tuple-element.21.w1_ref, ...), custom_call_target="tpu_custom_call" | custom-call | flops 47244640256 | bytes 10000000 | tf_op jit(solution)/shard_map/backward/pallas_call | solution.py:521
  235.5 0.0 copy-done.1
  235.5 0.0 copy-done.2
  235.5 1.9 pad_maximum_fusion
  237.5 0.0 copy-done
  237.5 1.7 pad_maximum_fusion.2
  239.2 4.5 %copy.10 = bf16[1,4096,512]{2,1,0:T(8,128)(2,1)} copy(bf16[1,4096,512]{2,1,0:T(8,128)(2,1)} %bitcast.9) | data formatting | bytes 8388608
Async XLA Ops:
  146.6 89.0 %copy-start.1 = (bf16[64,1408]{1,0:T(8,128)(2,1)S(1)}, bf16[64,1408]{1,0:T(8,128)(2,1)}, u32[]{:S(2)}) copy-start(bf16[64,1408]{1,0:T(8,128)(2,1)} %get-tuple-element.25) | copy-start | bytes 540676
  146.6 89.0 %copy-start.2 = (bf16[64,1408]{1,0:T(8,128)(2,1)S(1)}, bf16[64,1408]{1,0:T(8,128)(2,1)}, u32[]{:S(2)}) copy-start(bf16[64,1408]{1,0:T(8,128)(2,1)} %get-tuple-element.27) | copy-start | bytes 540676
  146.6 90.9 %copy-start = (bf16[176,512]{1,0:T(8,128)(2,1)S(1)}, bf16[176,512]{1,0:T(8,128)(2,1)}, u32[]{:S(2)}) copy-start(bf16[176,512]{1,0:T(8,128)(2,1)} %get-tuple-element.29) | copy-start | bytes 540676

commit v4 on v3

--- a/solution.py
+++ b/solution.py
@@ -11,6 +11,7 @@
 EPS = 1e-6
 BF, F32 = jnp.bfloat16, jnp.float32
 TM = 512
+TB = 1024
 CH = 256
 VMEM_LIMIT = 60 * 2**20
 
@@ -357,14 +358,14 @@
     )
     down = Scatter(dw2_ref, *scratch[2 * n :])
     before = [
-        (s2, first.begin), (s2 + 1, first.add_pair), (s2 + 4, lambda: first.add_relay(0)), (s2 + 6, lambda: first.add_relay(1)),
-        (s3, down.begin), (s3 + 2, down.add_pair), (s4 + 1, lambda: down.add_relay(0)), (s4 + 3, lambda: down.add_relay(1)),
-        (s4, second.begin), (s4 + 1, second.add_pair), (s4 + 6, lambda: second.add_relay(0)),
+        (s2, first.begin), (s2 + 1, first.send), (s2 + 3, lambda: first.send_relay(0)), (s3, lambda: first.send_relay(1)),
+        (s3, down.begin), (s3 + 1, down.send), (s4, lambda: down.send_relay(0)), (s4 + 1, lambda: down.send_relay(1)),
+        (s4, second.begin), (s4 + 1, second.send), (s4 + 3, lambda: second.send_relay(0)),
     ]
     after = [
-        (s2 + 1, first.send), (s2 + 4, lambda: first.send_relay(0)), (s2 + 6, lambda: first.send_relay(1)),
-        (s3 + 2, down.send), (s4 + 1, lambda: down.send_relay(0)), (s4 + 3, lambda: down.send_relay(1)),
-        (s4 + 1, second.send), (s4 + 6, lambda: second.send_relay(0)),
+        (s2, first.add_pair), (s2 + 2, lambda: first.add_relay(0)), (s2 + 3, lambda: first.add_relay(1)),
+        (s3, down.add_pair), (s4 - 1, lambda: down.add_relay(0)), (s4, lambda: down.add_relay(1)),
+        (s4, second.add_pair), (s4 + 2, lambda: second.add_relay(0)),
     ]
 
     def first_end():
@@ -377,13 +378,13 @@
             dgate_ref[:, s : s + w] = block[:, at : at + w]
             dup_ref[:, s : s + w] = block[:, at + w : at + 2 * w]
 
-    before.append((s3 + 1, first_end))
+    before.append((s4, first_end))
     pl.when(step == 0)(lambda: meet(z_peers() + [sibling()]))
     for at, do in before:
         pl.when(step == at)(do)
 
     def hidden(part, tile):
-        rows_of = pl.ds(pl.multiple_of(tile * TM, TM), TM)
+        rows_of = pl.ds(pl.multiple_of(tile * TB, TB), TB)
         wide = h_ref[...].astype(F32)
         a = (wide * scale_of(wide)).astype(BF)
         if part == 0:
@@ -428,7 +429,7 @@
 
     @pl.when(step >= s4)
     def _():
-        rows_of = pl.ds(pl.multiple_of((step - s4) * TM, TM), TM)
+        rows_of = pl.ds(pl.multiple_of((step - s4) * TB, TB), TB)
         da = dot_nt(dgu_ref[rows_of, :], w1_ref[...]).astype(BF).astype(F32)
         wide = h_ref[...].astype(F32)
         scale = scale_of(wide)
@@ -510,7 +511,7 @@
 def backward(h, by, w1, w2, number):
     t, d = h.shape
     ff = w2.shape[0]
-    tiles = t // TM
+    tiles = t // TB
     s1, s2, s3, s4, count = marks(tiles, ff)
 
     def tile(i):
@@ -520,11 +521,11 @@
     (_, cut), _ = halves(ff)
     return pl.pallas_call(
         functools.partial(backward_kernel, tiles), grid=(count,), name="backward",
-        in_specs=[pl.BlockSpec((TM, d), tile), pl.BlockSpec((TM, d), tile), once(w1.shape), once(w2.shape)],
-        out_specs=[pl.BlockSpec((TM, d), lambda i: (jnp.maximum(i - s4, 0), 0)), whole((r1, ff)), whole((r1, ff)), whole((r2, d))],
+        in_specs=[pl.BlockSpec((TB, d), tile), pl.BlockSpec((TB, d), tile), once(w1.shape), once(w2.shape)],
+        out_specs=[pl.BlockSpec((TB, d), lambda i: (jnp.maximum(i - s4, 0), 0)), whole((r1, ff)), whole((r1, ff)), whole((r2, d))],
         out_shape=shapes((t, d), (r1, ff), (r1, ff), (r2, d)),
         scratch_shapes=[
-            pltpu.VMEM((t, 2 * ff), BF), pltpu.VMEM((d, t), BF), pltpu.VMEM((TM, cut), BF), pltpu.VMEM((d, ff), F32),
+            pltpu.VMEM((t, 2 * ff), BF), pltpu.VMEM((d, t), BF), pltpu.VMEM((TB, cut), BF), pltpu.VMEM((d, ff), F32),
             pltpu.VMEM((d, 2 * ff), BF), pltpu.VMEM((ff, d), BF),
             *Scatter.scratch(r1, 2 * cut), *Scatter.scratch(r1, 2 * (ff - cut)), *Scatter.scratch(r2, d),
         ],

time: 244 us -> 225 us (0.922)
  Pallas kernels: 235 us -> 215 us
    pallas_call x2, Pallas kernels: 177 us -> 157 us  [backward(): pl.pallas_call(functools.partial(backward_kernel, tiles), grid=(count,),...]
where the time goes in v4:
time: 225 us; the launch traced here: 224 us
  Pallas kernels  215 us (96%)
  local copies, waits for them, and re-layouts  4.48 us (2%)
  other arithmetic  3.63 us (2%)
    pallas_call x2, Pallas kernels, backward(): pl.pallas_call(functools.partial(backward_kernel, tiles), grid=(count,),...  157 us
    pallas_call x1, Pallas kernels, forward(): pl.pallas_call(functools.partial(forward_kernel, tiles), grid=(2 * tiles,...  57.4 us

profile of v4, /device:TPU:0, one launch (start us, length us, event | category | flops | bytes accessed | tf_op | source)
XLA Modules:
  0.0 223.6 jit_solution(18114251183791051560)
XLA Ops:
  0.6 57.4 %forward.1 = (bf16[4096,512]{1,0:T(8,128)(2,1)}, bf16[512,2816]{1,0:T(8,128)(2,1)}, bf16[1408,512]{1,0:T(8,128)(2,1)}, bf16[512,2816]{1,0:T(8,128)(2,1)}, bf16[1408,512]{1,0:T(8,128)(2,1)}) custom-call(bf16[4096,512]{1,0:T(8,128)(2,1)} %bitcast.17, bf16[2,64,1408]{2,1,0:T(8,128)(2,1)} %next_gates.1, bf16[2,64,1408]{2,1,0:T(8,128)(2,1)} %next_ups.1, ...), custom_call_target="tpu_custom_call" | custom-call | flops 17716740096 | bytes 8388608 | tf_op jit(solution)/shard_map/forward/pallas_call | solution.py:494
  58.0 77.7 %backward.2 = (bf16[4096,512]{1,0:T(8,128)(2,1)}, bf16[64,1408]{1,0:T(8,128)(2,1)}, bf16[64,1408]{1,0:T(8,128)(2,1)}, bf16[176,512]{1,0:T(8,128)(2,1)}) custom-call(bf16[4096,512]{1,0:T(8,128)(2,1)} %get-tuple-element.17.h_ref, bf16[4096,512]{1,0:T(8,128)(2,1)} %bitcast.16, bf16[512,2816]{1,0:T(8,128)(2,1)} %get-tuple-element.18.w1_ref, ...), custom_call_target="tpu_custom_call" | custom-call | flops 47244640256 | bytes 10000000 | tf_op jit(solution)/shard_map/backward/pallas_call | solution.py:522
  135.7 0.0 copy-start.1
  135.7 0.0 copy-start.2
  135.7 0.0 copy-start
  135.7 79.8 %backward.3 = (bf16[4096,512]{1,0:T(8,128)(2,1)}, bf16[64,1408]{1,0:T(8,128)(2,1)}, bf16[64,1408]{1,0:T(8,128)(2,1)}, bf16[176,512]{1,0:T(8,128)(2,1)}) custom-call(bf16[4096,512]{1,0:T(8,128)(2,1)} %bitcast.18, bf16[4096,512]{1,0:T(8,128)(2,1)} %get-tuple-element.20.by_ref, bf16[512,2816]{1,0:T(8,128)(2,1)} %get-tuple-element.21.w1_ref, ...), custom_call_target="tpu_custom_call" | custom-call | flops 47244640256 | bytes 10000000 | tf_op jit(solution)/shard_map/backward/pallas_call | solution.py:522
  215.5 0.0 copy-done.1
  215.5 0.0 copy-done.2
  215.5 1.9 pad_maximum_fusion
  217.5 0.0 copy-done
  217.5 1.7 pad_maximum_fusion.2
  219.2 4.5 %copy.10 = bf16[1,4096,512]{2,1,0:T(8,128)(2,1)} copy(bf16[1,4096,512]{2,1,0:T(8,128)(2,1)} %bitcast.9) | data formatting | bytes 8388608
Async XLA Ops:
  135.7 79.9 %copy-start.1 = (bf16[64,1408]{1,0:T(8,128)(2,1)S(1)}, bf16[64,1408]{1,0:T(8,128)(2,1)}, u32[]{:S(2)}) copy-start(bf16[64,1408]{1,0:T(8,128)(2,1)} %get-tuple-element.25) | copy-start | bytes 540676
  135.7 79.9 %copy-start.2 = (bf16[64,1408]{1,0:T(8,128)(2,1)S(1)}, bf16[64,1408]{1,0:T(8,128)(2,1)}, u32[]{:S(2)}) copy-start(bf16[64,1408]{1,0:T(8,128)(2,1)} %get-tuple-element.27) | copy-start | bytes 540676
  135.7 81.8 %copy-start = (bf16[176,512]{1,0:T(8,128)(2,1)S(1)}, bf16[176,512]{1,0:T(8,128)(2,1)}, u32[]{:S(2)}) copy-start(bf16[176,512]{1,0:T(8,128)(2,1)} %get-tuple-element.29) | copy-start | bytes 540676

commit v5 on v4

--- a/solution.py
+++ b/solution.py
@@ -10,8 +10,7 @@
 
 EPS = 1e-6
 BF, F32 = jnp.bfloat16, jnp.float32
-TM = 512
-TB = 1024
+TM = 1024
 CH = 256
 VMEM_LIMIT = 60 * 2**20
 
@@ -312,11 +311,13 @@
         w1.arrived()
         out[0].start()
 
+    def each(do):
+        for i in ORDER:
+            do(i)
+
     for at, do in (
-        (1, lambda: [w2.pass_in(2), next_w1.hand_on(2)]), (2, lambda: [w2.pass_in(1), next_w1.hand_on(1)]),
-        (3, lambda: [w2.pass_in(3), next_w1.hand_on(3)]), (4, lambda: next_w2.hand_on(2)), (5, lambda: next_w2.hand_on(1)),
-        (6, lambda: next_w2.hand_on(3)), (8, lambda: [w2.arrived(), out[1].start()]), (9, lambda: next_w1.pass_in(2)),
-        (10, lambda: next_w1.pass_in(1)), (11, lambda: next_w1.pass_in(3)), (13, lambda: next_w2.pass_in(2)), (14, lambda: next_w2.pass_in(1)),
+        (1, lambda: [each(w2.pass_in), each(next_w1.hand_on)]), (2, lambda: each(next_w2.hand_on)),
+        (tiles, lambda: [w2.arrived(), out[1].start()]), (tiles + 2, lambda: each(next_w1.pass_in)),
     ):
         pl.when(step == at)(lambda do=do: do() and None)
 
@@ -338,7 +339,7 @@
 
     @pl.when(step == 2 * tiles - 1)
     def _():
-        next_w2.pass_in(3)
+        each(next_w2.pass_in)
         later.arrived()
         now.sent()
         later.sent()
@@ -346,7 +347,9 @@
             c.wait()
 
 
-def backward_kernel(tiles, h_ref, by_ref, w1_ref, w2_ref, o_ref, dgate_ref, dup_ref, ddown_ref, dgu_ref, at_ref, p_ref, acc_ref, dw1_ref, dw2_ref, *scratch):
+def backward_kernel(tiles, kept, h_ref, by_ref, w1_ref, w2_ref, *refs):
+    others, (o_ref, *grads, dgu_ref, at_ref, p_ref, acc_ref, dw1_ref, dw2_ref), scratch = refs[:kept], refs[kept : kept + 10], refs[kept + 10 :]
+    dgate_ref, dup_ref, ddown_ref = (g.at[0] for g in grads)
     ff = w2_ref.shape[0]
     parts = halves(ff)
     runs = [[c for c in chunks(ff) if lo <= c[0] < hi] for lo, hi in parts]
@@ -380,11 +383,17 @@
 
     before.append((s4, first_end))
     pl.when(step == 0)(lambda: meet(z_peers() + [sibling()]))
+
+    @pl.when(step == 1)
+    def _():
+        for other, grad in zip(others, grads):
+            grad[1:] = other[...]
+
     for at, do in before:
         pl.when(step == at)(do)
 
     def hidden(part, tile):
-        rows_of = pl.ds(pl.multiple_of(tile * TB, TB), TB)
+        rows_of = pl.ds(pl.multiple_of(tile * TM, TM), TM)
         wide = h_ref[...].astype(F32)
         a = (wide * scale_of(wide)).astype(BF)
         if part == 0:
@@ -429,7 +438,7 @@
 
     @pl.when(step >= s4)
     def _():
-        rows_of = pl.ds(pl.multiple_of((step - s4) * TB, TB), TB)
+        rows_of = pl.ds(pl.multiple_of((step - s4) * TM, TM), TM)
         da = dot_nt(dgu_ref[rows_of, :], w1_ref[...]).astype(BF).astype(F32)
         wide = h_ref[...].astype(F32)
         scale = scale_of(wide)
@@ -508,10 +517,10 @@
     return pl.BlockSpec(shape, lambda i: (0,) * len(shape), pipeline_mode=pl.Buffered(buffer_count=1))
 
 
-def backward(h, by, w1, w2, number):
+def backward(h, by, w1, w2, number, others=()):
     t, d = h.shape
     ff = w2.shape[0]
-    tiles = t // TB
+    tiles = t // TM
     s1, s2, s3, s4, count = marks(tiles, ff)
 
     def tile(i):
@@ -519,18 +528,20 @@
 
     r1, r2 = d // 8, ff // 8
     (_, cut), _ = halves(ff)
+    count_of = 1 + sum(t.shape[0] for t in others[:1])
+    blocks = [(count_of, r1, ff), (count_of, r1, ff), (count_of, r2, d)]
     return pl.pallas_call(
-        functools.partial(backward_kernel, tiles), grid=(count,), name="backward",
-        in_specs=[pl.BlockSpec((TB, d), tile), pl.BlockSpec((TB, d), tile), once(w1.shape), once(w2.shape)],
-        out_specs=[pl.BlockSpec((TB, d), lambda i: (jnp.maximum(i - s4, 0), 0)), whole((r1, ff)), whole((r1, ff)), whole((r2, d))],
-        out_shape=shapes((t, d), (r1, ff), (r1, ff), (r2, d)),
+        functools.partial(backward_kernel, tiles, len(others)), grid=(count,), name="backward",
+        in_specs=[pl.BlockSpec((TM, d), tile), pl.BlockSpec((TM, d), tile), once(w1.shape), once(w2.shape), *(once(t.shape) for t in others)],
+        out_specs=[pl.BlockSpec((TM, d), lambda i: (jnp.maximum(i - s4, 0), 0)), *(once(b) for b in blocks)],
+        out_shape=shapes((t, d), *blocks),
         scratch_shapes=[
-            pltpu.VMEM((t, 2 * ff), BF), pltpu.VMEM((d, t), BF), pltpu.VMEM((TB, cut), BF), pltpu.VMEM((d, ff), F32),
+            pltpu.VMEM((t, 2 * ff), BF), pltpu.VMEM((d, t), BF), pltpu.VMEM((TM, cut), BF), pltpu.VMEM((d, ff), F32),
             pltpu.VMEM((d, 2 * ff), BF), pltpu.VMEM((ff, d), BF),
             *Scatter.scratch(r1, 2 * cut), *Scatter.scratch(r1, 2 * (ff - cut)), *Scatter.scratch(r2, d),
         ],
         compiler_params=params(number), cost_estimate=cost(16 * t * d * ff, 10**7),
-    )(h, by, w1, w2)
+    )(h, by, w1, w2, *others)
 
 
 def solution(mesh):
@@ -539,8 +550,8 @@
         blocks = (w_gate, w_up, w_down)
         h, w1, w2, v1, v2 = forward(x, blocks, 1)
         by, *last = backward(h, by, v1, v2, 2)
-        by, *first = backward(x, by, w1, w2, 3)
-        return (by[None], *(jnp.stack(pair) for pair in zip(first, last)))
+        by, *both = backward(x, by, w1, w2, 3, last)
+        return (by[None], *both)
 
     spread, by_rows = P(("rep", "dp"), None, None), P(None, "dp", None)
     group = P("rep", "dp", None)

time: 225 us -> 222 us (0.987)
  other arithmetic: 3.63 us -> 0 us
  local copies, waits for them, and re-layouts: 4.48 us -> 6.77 us
    another operation x2 -> x0, other arithmetic: 3.63 us -> none  [step(): return (by[None], *(jnp.stack(pair) for pair in zip(first, last)))]
    unnamed x7 -> x10, local copies, waits for them, and re-layouts: 4.48 us -> 6.77 us
where the time goes in v5:
time: 222 us; the launch traced here: 221 us
  Pallas kernels  213 us (96%)
  local copies, waits for them, and re-layouts  6.77 us (3%)
    pallas_call x2, Pallas kernels, backward(): pl.pallas_call(functools.partial(backward_kernel, tiles, len(others)), gr...  157 us
    pallas_call x1, Pallas kernels, forward(): pl.pallas_call(functools.partial(forward_kernel, tiles), grid=(2 * tiles,...  55.8 us
    unnamed x10, local copies, waits for them, and re-layouts  6.77 us

profile of v5, /device:TPU:0, one launch (start us, length us, event | category | flops | bytes accessed | tf_op | source)
XLA Modules:
  0.0 220.7 jit_solution(273680924597398177)
XLA Ops:
  0.6 55.8 %forward.1 = (bf16[4096,512]{1,0:T(8,128)(2,1)}, bf16[512,2816]{1,0:T(8,128)(2,1)}, bf16[1408,512]{1,0:T(8,128)(2,1)}, bf16[512,2816]{1,0:T(8,128)(2,1)}, bf16[1408,512]{1,0:T(8,128)(2,1)}) custom-call(bf16[4096,512]{1,0:T(8,128)(2,1)} %bitcast.5, bf16[2,64,1408]{2,1,0:T(8,128)(2,1)} %next_gates.1, bf16[2,64,1408]{2,1,0:T(8,128)(2,1)} %next_ups.1, ...), custom_call_target="tpu_custom_call" | custom-call | flops 17716740096 | bytes 8388608 | tf_op jit(solution)/shard_map/forward/pallas_call | solution.py:503
  56.4 77.1 %backward.2 = (bf16[4096,512]{1,0:T(8,128)(2,1)}, bf16[1,64,1408]{2,1,0:T(8,128)(2,1)}, bf16[1,64,1408]{2,1,0:T(8,128)(2,1)}, bf16[1,176,512]{2,1,0:T(8,128)(2,1)}) custom-call(bf16[4096,512]{1,0:T(8,128)(2,1)} %get-tuple-element.17.h_ref, bf16[4096,512]{1,0:T(8,128)(2,1)} %bitcast.4, bf16[512,2816]{1,0:T(8,128)(2,1)} %get-tuple-element.18.w1_ref, ...), custom_call_target="tpu_custom_call" | custom-call | flops 47244640256 | bytes 10000000 | tf_op jit(solution)/shard_map/backward/pallas_call | solution.py:533
  133.5 80.3 %backward.3 = (bf16[4096,512]{1,0:T(8,128)(2,1)}, bf16[2,64,1408]{2,1,0:T(8,128)(2,1)}, bf16[2,64,1408]{2,1,0:T(8,128)(2,1)}, bf16[2,176,512]{2,1,0:T(8,128)(2,1)}) custom-call(bf16[4096,512]{1,0:T(8,128)(2,1)} %bitcast.6, bf16[4096,512]{1,0:T(8,128)(2,1)} %get-tuple-element.20.by_ref, bf16[512,2816]{1,0:T(8,128)(2,1)} %get-tuple-element.21.w1_ref, ...), custom_call_target="tpu_custom_call" | custom-call | flops 47244640256 | bytes 10000000 | tf_op jit(solution)/shard_map/backward/pallas_call | solution.py:533
  213.9 0.0 copy-start.2
  213.9 0.0 copy-start.1
  213.9 0.0 copy-start
  213.9 4.6 %copy.13 = bf16[1,4096,512]{2,1,0:T(8,128)(2,1)} copy(bf16[1,4096,512]{2,1,0:T(8,128)(2,1)} %bitcast.3) | data formatting | bytes 8388608
  218.5 0.0 copy-done.2
  218.5 0.7 copy.14
  219.2 0.0 copy-done.1
  219.2 0.7 copy.15
  219.9 0.0 copy-done
  219.9 0.7 copy.16
Async XLA Ops:
  213.9 4.6 %copy-start.2 = (bf16[2,64,1408]{2,1,0:T(8,128)(2,1)S(1)}, bf16[2,64,1408]{2,1,0:T(8,128)(2,1)}, u32[]{:S(2)}) copy-start(bf16[2,64,1408]{2,1,0:T(8,128)(2,1)} %get-tuple-element.35) | copy-start | bytes 1081348
  213.9 5.3 %copy-start.1 = (bf16[2,64,1408]{2,1,0:T(8,128)(2,1)S(1)}, bf16[2,64,1408]{2,1,0:T(8,128)(2,1)}, u32[]{:S(2)}) copy-start(bf16[2,64,1408]{2,1,0:T(8,128)(2,1)} %get-tuple-element.36) | copy-start | bytes 1081348
  213.9 6.0 %copy-start = (bf16[2,176,512]{2,1,0:T(8,128)(2,1)S(1)}, bf16[2,176,512]{2,1,0:T(8,128)(2,1)}, u32[]{:S(2)}) copy-start(bf16[2,176,512]{2,1,0:T(8,128)(2,1)} %get-tuple-element.37) | copy-start | bytes 1081348

commit v6 on v5

--- a/solution.py
+++ b/solution.py
@@ -108,6 +108,14 @@
         own = (self.shard.at[pl.ds(pl.multiple_of(rep * n, n), n), :], self.down.at[0, :, pl.ds(pl.multiple_of(rep * self.cols, self.cols), self.cols)])
         return self.copies(i - 1, own, self.quarter(z, core, rep), (rep, (z + i) % Z, core))
 
+    def diagonal(self, i):
+        rep, z, core = place()
+        odd, q = rep % 2, 3 - rep
+        src = self.down.at[0, :, pl.ds(pl.multiple_of(q * self.cols, self.cols), self.cols)]
+        number = 3 + 3 * (i - 1) - 1
+        sems = self.send_sems.at[2 * (number + 3 - 2 * odd) + 1], self.recv_sems.at[2 * (number + 1 + 2 * odd) + 1]
+        return remote(src, self.quarter(z, core, q)[1], *sems, rep, (z + i) % Z, core)
+
     def across(self, i, j):
         rep, z, core = place()
         part = self.quarter((z + Z - i) % Z, core, rep)
@@ -136,15 +144,22 @@
         for i in (2, 1, 3):
             for c in self.along_z(i):
                 c.start()
+        if 1 in self.which:
+            for i in (2, 1, 3):
+                self.diagonal(i).start()
         for c in self.inside_own() + self.keep_own():
             c.start()
 
     def hand_on(self, i):
         for c in self.along_z(i):
             c.wait_recv()
+        rep, _, _ = place()
         for j in range(1, 4):
-            for c in self.across(i, j):
-                c.start()
+            for which, c in zip(self.which, self.across(i, j)):
+                if which == 0 or j == 2:
+                    c.start()
+                else:
+                    pl.when(j != 3 - 2 * (rep % 2))(c.start)
         for c in self.inside(i, 0):
             c.start()
 

time: 222 us -> 224 us (level)
  no operation moved by 1% of the time
where the time goes in v6:
time: 224 us; the launch traced here: 222 us
  Pallas kernels  215 us (96%)
  local copies, waits for them, and re-layouts  6.77 us (3%)
    pallas_call x2, Pallas kernels, backward(): pl.pallas_call(functools.partial(backward_kernel, tiles, len(others)), gr...  159 us
    pallas_call x1, Pallas kernels, forward(): pl.pallas_call(functools.partial(forward_kernel, tiles), grid=(2 * tiles,...  56.2 us
    unnamed x10, local copies, waits for them, and re-layouts  6.77 us

profile of v6, /device:TPU:0, one launch (start us, length us, event | category | flops | bytes accessed | tf_op | source)
XLA Modules:
  0.0 222.2 jit_solution(1162672944358363195)
XLA Ops:
  0.6 56.2 %forward.1 = (bf16[4096,512]{1,0:T(8,128)(2,1)}, bf16[512,2816]{1,0:T(8,128)(2,1)}, bf16[1408,512]{1,0:T(8,128)(2,1)}, bf16[512,2816]{1,0:T(8,128)(2,1)}, bf16[1408,512]{1,0:T(8,128)(2,1)}) custom-call(bf16[4096,512]{1,0:T(8,128)(2,1)} %bitcast.5, bf16[2,64,1408]{2,1,0:T(8,128)(2,1)} %next_gates.1, bf16[2,64,1408]{2,1,0:T(8,128)(2,1)} %next_ups.1, ...), custom_call_target="tpu_custom_call" | custom-call | flops 17716740096 | bytes 8388608 | tf_op jit(solution)/shard_map/forward/pallas_call | solution.py:518
  56.8 78.2 %backward.2 = (bf16[4096,512]{1,0:T(8,128)(2,1)}, bf16[1,64,1408]{2,1,0:T(8,128)(2,1)}, bf16[1,64,1408]{2,1,0:T(8,128)(2,1)}, bf16[1,176,512]{2,1,0:T(8,128)(2,1)}) custom-call(bf16[4096,512]{1,0:T(8,128)(2,1)} %get-tuple-element.17.h_ref, bf16[4096,512]{1,0:T(8,128)(2,1)} %bitcast.4, bf16[512,2816]{1,0:T(8,128)(2,1)} %get-tuple-element.18.w1_ref, ...), custom_call_target="tpu_custom_call" | custom-call | flops 47244640256 | bytes 10000000 | tf_op jit(solution)/shard_map/backward/pallas_call | solution.py:548
  135.0 80.3 %backward.3 = (bf16[4096,512]{1,0:T(8,128)(2,1)}, bf16[2,64,1408]{2,1,0:T(8,128)(2,1)}, bf16[2,64,1408]{2,1,0:T(8,128)(2,1)}, bf16[2,176,512]{2,1,0:T(8,128)(2,1)}) custom-call(bf16[4096,512]{1,0:T(8,128)(2,1)} %bitcast.6, bf16[4096,512]{1,0:T(8,128)(2,1)} %get-tuple-element.20.by_ref, bf16[512,2816]{1,0:T(8,128)(2,1)} %get-tuple-element.21.w1_ref, ...), custom_call_target="tpu_custom_call" | custom-call | flops 47244640256 | bytes 10000000 | tf_op jit(solution)/shard_map/backward/pallas_call | solution.py:548
  215.3 0.0 copy-start.2
  215.4 0.0 copy-start.1
  215.4 0.0 copy-start
  215.4 4.6 %copy.13 = bf16[1,4096,512]{2,1,0:T(8,128)(2,1)} copy(bf16[1,4096,512]{2,1,0:T(8,128)(2,1)} %bitcast.3) | data formatting | bytes 8388608
  219.9 0.0 copy-done.2
  219.9 0.7 copy.14
  220.7 0.0 copy-done.1
  220.7 0.7 copy.15
  221.4 0.0 copy-done
  221.4 0.7 copy.16
Async XLA Ops:
  215.3 4.6 %copy-start.2 = (bf16[2,64,1408]{2,1,0:T(8,128)(2,1)S(1)}, bf16[2,64,1408]{2,1,0:T(8,128)(2,1)}, u32[]{:S(2)}) copy-start(bf16[2,64,1408]{2,1,0:T(8,128)(2,1)} %get-tuple-element.35) | copy-start | bytes 1081348
  215.4 5.3 %copy-start.1 = (bf16[2,64,1408]{2,1,0:T(8,128)(2,1)S(1)}, bf16[2,64,1408]{2,1,0:T(8,128)(2,1)}, u32[]{:S(2)}) copy-start(bf16[2,64,1408]{2,1,0:T(8,128)(2,1)} %get-tuple-element.36) | copy-start | bytes 1081348
  215.4 6.0 %copy-start = (bf16[2,176,512]{2,1,0:T(8,128)(2,1)S(1)}, bf16[2,176,512]{2,1,0:T(8,128)(2,1)}, u32[]{:S(2)}) copy-start(bf16[2,176,512]{2,1,0:T(8,128)(2,1)} %get-tuple-element.37) | copy-start | bytes 1081348
